TPU v7x, 256 devices: a whole 4x4x8 slice. The times are simulated.
256 devices in a mesh: batch: 32 (over x, z_hi, core), hidden: 8 (over z_lo, y).
Axes of the slice: x: 4, y: 4, z: 8 (z_hi: 4, z_lo: 2; z = z_hi * 2 + z_lo), core: 2. Of those that a mesh axis runs over, the one named last changes fastest.
Arguments:
- features: bfloat16 [12288, 512], P('batch'), may hold values from -6 to 6
- w_first: bfloat16 [512, 8192], P('batch', 'hidden'), may hold values from -0.25 to 0.25
- w_second: bfloat16 [8192, 4096], P('hidden', 'batch'), may hold values from -0.0625 to 0.0625
- w_head: bfloat16 [4096, 8], P('hidden'), may hold values from -0.09375 to 0.09375
- rewards: float32 [8, 12288], P(None, 'batch'), may hold values from -1.75 to 1.75
- discount: float32 [8], replicated, as said below
- trace: float32 [8], replicated, as said below
- episode: int32 [12288], P('batch'), may hold values from 0 to 32, as said below
Outputs:
- advantages: float32 [8, 12288], P(None, 'batch')
- loss: float32 [], replicated
- grad_first: float32 [512, 8192], P('batch', 'hidden')
- grad_second: float32 [8192, 4096], P('hidden', 'batch')
- grad_head: float32 [4096, 8], P('hidden')
Inputs may be any that keep to these rules, and one draw needn't show every extreme that they name: Each discount lies between 0.875 and 1. Each trace factor lies between 0.875 and 1. episode numbers never fall along the rollout and rise by one at each episode start; each block of 384 timesteps of one index of batch holds exactly one episode start besides the rollout's own start at timestep 0, and that start never falls on the block's first timestep; the rollout begins with episode 0.
All inputs are finite; a program needn't handle non-finite values.
Results may differ from a plain program's by a relative error of at most 0.018.
Values may be sent and summed in bfloat16 or wider, within the bound.
A program may use at most 128 MiB of HBM per device.

v0:
```python
import jax
import jax.numpy as jnp
from jax import lax
from jax.sharding import PartitionSpec as P


def sent_to_all(array, axis):
    length = lax.axis_size(axis)
    return lax.all_to_all(
        jnp.broadcast_to(array[None], (length, *array.shape)), axis, 0, 0, tiled=True
    )


def over_copies(array, axis):
    return sent_to_all(array, axis).sum(axis=0)


def passed_along(value, axis, steps):
    count = lax.axis_size(axis)
    initial, last = (max(0, -steps), min(count, count - steps))
    return lax.ppermute(value, axis, [(source, source + steps) for source in range(initial, last)])


def collected_together(array, axis):
    leaves = jax.tree.leaves(array)
    turns = sorted(range(len(leaves)), key=lambda k: -leaves[k].size)
    width = (1, *leaves[turns[0]].shape)[-1]
    lines = [
        jnp.pad(leaves[k].reshape(-1), (0, -leaves[k].size % width)).reshape(-1, width)
        for k in turns
    ]
    both, at, found = (sent_to_all(jnp.concatenate(lines), axis), 0, {})
    for k, line in zip(turns, lines):
        share = both[:, at : at + len(line)].reshape(len(both), -1)
        found[k] = share[:, : leaves[k].size].reshape(-1, *leaves[k].shape)
        at += len(line)
    numbers = iter(range(len(leaves)))
    return jax.tree.map(lambda _: found[next(numbers)], array)


def joined_by_halves(pieces, combine):
    while len(jax.tree.leaves(pieces)[0]) > 1:
        pieces = jax.vmap(combine)(
            *(jax.tree.map(lambda part: part[side::2], pieces) for side in (0, 1))
        )
    return jax.tree.map(lambda part: part[0], pieces)


def prefix(array, axis, combine, identity):
    length, position = (lax.axis_size(axis), lax.axis_index(axis))
    passed = jnp.arange(length) > position

    def kept(part, zero, own):
        part = jnp.where(
            passed.reshape(-1, *(1 for _ in own.shape)), part, jnp.asarray(zero, own.dtype)
        )
        return part[::-1]

    pieces = collected_together(array, axis)
    return joined_by_halves(jax.tree.map(kept, pieces, identity, array), combine)


def cut_along(array, dim, length):
    before, after = (array.shape[:dim], array.shape[dim + 1 :])
    return jnp.moveaxis(array.reshape(*before, length, -1, *after), dim, 0)


def summed_on_arrival(array, axis, dim):
    length = lax.axis_size(axis)
    pieces = lax.all_to_all(cut_along(array, dim, length), axis, 0, 0, tiled=True)
    return jnp.sum(pieces.astype(jnp.float32), axis=0)


def chain_maps(farther, nearer):
    return (farther[0] * nearer[0], nearer[1] + nearer[0] * farther[1])


def silu_slope(value):
    sigmoid_value = jax.nn.sigmoid(value)
    return sigmoid_value * (1.0 + value * (1.0 - sigmoid_value))


def contract(left, right, left_dim, right_dim):
    return lax.dot_general(
        left, right, (((left_dim,), (right_dim,)), ((), ())), preferred_element_type=jnp.float32
    )


def shards(features, w_first, w_second, w_head, rewards, discount, trace, episode):
    rows_here = features.shape[0]
    heads = w_head.shape[1]
    columns = features
    pre_first = jnp.dot(
        columns,
        lax.all_gather(w_first, "batch", axis=0, tiled=True),
        preferred_element_type=jnp.float32,
    )
    hidden_first = jax.nn.silu(pre_first).astype(jnp.bfloat16)
    partial_value = jnp.dot(
        hidden_first,
        lax.all_gather(w_second, "batch", axis=1, tiled=True),
        preferred_element_type=jnp.float32,
    )
    pre_second = lax.psum_scatter(
        partial_value.astype(jnp.bfloat16), "hidden", scatter_dimension=1, tiled=True
    ).astype(jnp.float32)
    hidden_second = jax.nn.silu(pre_second).astype(jnp.bfloat16)
    values = over_copies(
        jnp.dot(hidden_second, w_head, preferred_element_type=jnp.float32), "hidden"
    )
    values_t = values.T
    next_value = passed_along(values_t[:, :1], "batch", -1)
    next_first = passed_along(episode[:1] + 1, "batch", -1)
    following = jnp.concatenate([episode[1:] + 1, next_first])
    keep = (following == episode + 1).astype(jnp.float32)
    value_after = jnp.concatenate([values_t[:, 1:], next_value], axis=1)
    delta = rewards + discount[:, None] * keep[None, :] * value_after - values_t
    factor = discount[:, None] * trace[:, None] * keep[None, :]
    reach, local_adv = lax.associative_scan(chain_maps, (factor, delta), reverse=True, axis=1)
    identity = (jnp.ones((heads,), jnp.float32), jnp.zeros((heads,), jnp.float32))
    _, entering = prefix((reach[:, 0], local_adv[:, 0]), "batch", chain_maps, identity)
    advantages = local_adv + reach * entering[:, None]
    slope_value = (-advantages.T).astype(jnp.bfloat16)
    slope_share = (contract(slope_value, w_head, 1, 1) * silu_slope(pre_second)).astype(
        jnp.bfloat16
    )
    slope_second = lax.all_gather(slope_share, "hidden", axis=1, tiled=True)
    head_term = contract(hidden_second, slope_value, 0, 0)
    grad_head, loss_sum = (
        over_copies(head_term, "batch"),
        over_copies(jnp.sum(advantages * advantages), "batch"),
    )
    loss = 0.5 * loss_sum / (rows_here * lax.axis_size("batch") * heads)
    columns = slope_second
    back_first = contract(columns, lax.all_gather(w_second, "batch", axis=1, tiled=True), 1, 1)
    slope_first = (back_first * silu_slope(pre_first)).astype(jnp.bfloat16)
    columns = slope_second
    grad_second = (
        lax.psum_scatter(
            contract(columns, hidden_first, 0, 0).astype(jnp.bfloat16),
            "batch",
            scatter_dimension=0,
            tiled=True,
        )
        .astype(jnp.float32)
        .T
    )
    columns = features
    grad_first = summed_on_arrival(
        contract(columns, slope_first, 0, 0).astype(jnp.bfloat16), "batch", 0
    )
    return (advantages, loss, grad_first, grad_second, grad_head)


def solution(mesh):
    placed = (
        P("batch", None),
        P("batch", "hidden"),
        P("hidden", "batch"),
        P("hidden", None),
        P(None, "batch"),
        P(),
        P(),
        P("batch"),
    )
    return jax.shard_map(
        shards,
        mesh=mesh,
        in_specs=placed,
        out_specs=(
            P(None, "batch"),
            P(),
            P("batch", "hidden"),
            P("hidden", "batch"),
            P("hidden", None),
        ),
        check_vma=False,
    )
```

profile of v0, /device:TPU:1, one launch (start us, length us, event | category | flops | bytes accessed | tf_op | source)
XLA Modules:
  0.0 450.0 jit_solution(7222530237722029714)
XLA Ops:
  7.2 0.7 all-gather.4.cloned.1.call-update
  8.0 0.7 all-gather.6.cloned.1.call-update
  8.7 58.0 %all-gather.4.cloned.1.call-done = bf16[512,1024]{1,0:T(8,128)(2,1)} async-done(((bf16[16,1024]{1,0:T(8,128)(2,1)}), bf16[512,1024]{1,0:T(8,128)(2,1)}) %all-gather.4.cloned.1.call-update) | async-done | bytes 1048592 | tf_op jit(solution)/shard_map/all_gather | solution.py:95
  66.7 1.8 fusion.20
  68.5 82.7 %all-gather.6.cloned.1.call-done = bf16[1024,4096]{1,0:T(8,128)(2,1)} async-done(((bf16[1024,128]{1,0:T(8,128)(2,1)}), bf16[1024,4096]{1,0:T(8,128)(2,1)}) %all-gather.6.cloned.1.call-update) | async-done | bytes 8388624 | tf_op jit(solution)/shard_map/all_gather | solution.py:101
  151.2 8.2 %convolution_convert_fusion.1 = bf16[384,4096]{1,0:T(8,128)(2,1)} fusion(bf16[1024,4096]{1,0:T(8,128)(2,1)} %all-gather.6.cloned.1.call-done, f32[384,1024]{1,0:T(8,128)S(1)} %fusion.20), kind=kOutput, calls=%fused_computation.1 | convolution fusion | flops 3224764416 | bytes 13107200 | tf_op jit(solution)/shard_map/dot_general | solution.py:99
  159.4 0.6 copy-done.5
  160.1 0.5 slice.355
  161.3 3.1 collective-permute-start
  164.4 38.1 %reduce-scatter.3.cloned.1.call-done = bf16[384,512]{1,0:T(8,128)(2,1)} async-done(((bf16[384,4096]{1,0:T(8,128)(2,1)}), bf16[384,512]{1,0:T(8,128)(2,1)}) %reduce-scatter.3.cloned.1.call-update) | async-done | bytes 393232 | tf_op jit(solution)/shard_map/reduce_scatter | solution.py:104
  202.6 1.2 fusion.4
  203.8 0.2 fusion.21
  204.0 0.7 broadcast_in_dim.26
  204.7 3.9 all-to-all-start
  208.6 0.6 fusion.12
  209.2 4.7 %all-to-all-done = f32[8,384,8]{1,2,0:T(8,128)S(1)} async-done(((f32[8,384,8]{1,2,0:T(8,128)}), f32[8,384,8]{1,2,0:T(8,128)S(1)}, u32[]{:S(2)}, u32[]{:S(2)}) %all-to-all-start) | async-done | bytes 98336 | tf_op jit(solution)/shard_map/all_to_all | solution.py:9
  214.0 7.3 %collective-permute-start.1 = (f32[8,1]{1,0:T(8,128)S(1)}, f32[8,1]{1,0:T(8,128)S(1)}, u32[]{:S(2)}, u32[]{:S(2)}) collective-permute-start(f32[8,1]{1,0:T(8,128)S(1)} %slice.468), channel_id=1, source_target_pairs={{8,0},{16,8},{24,16},{32,24},{40,32},{48,40},{56,48},{64,56},{72,6... | collective-permute-start | bytes 104 | tf_op jit(solution)/shard_map/ppermute | solution.py:21
  221.3 3.3 collective-permute-done.1
  224.8 0.3 slice.371
  225.1 0.3 slice.365
  225.3 0.3 slice.361
  225.6 0.2 reverse.19
  226.0 0.2 slice.379
  226.2 0.2 slice.375
  226.3 0.2 slice.373
  226.6 0.3 slice.367
  226.9 0.3 slice.363
  227.1 0.3 slice.359
  227.4 0.2 reverse.18
  227.8 0.2 slice.376
  228.0 0.2 slice.374
  231.0 0.2 slice.370
  231.2 0.2 reverse.15
  235.1 0.2 pad.126
  235.5 0.3 pad.113
  236.0 0.3 pad.128
  236.4 0.3 pad.112
  236.7 0.3 pad.129
  237.0 0.2 add_reduce_fusion
  237.1 0.2 add_reduce_fusion.1
  237.3 0.6 broadcast_in_dim.28
  238.0 7.1 %all-to-all-start.1 = ((f32[32,2,8]{2,1,0:T(2,128)}), f32[32,2,8]{2,1,0:T(2,128)S(1)}, u32[]{:S(2)}, u32[]{:S(2)}) async-start(f32[32,2,8]{2,1,0:T(2,128)} %broadcast_in_dim.28), calls=%async_computation.2 | async-start | bytes 65536 | tf_op jit(solution)/shard_map/all_to_all | solution.py:9
  245.2 0.2 rev.4
  245.4 0.2 rev.5
  245.7 9.1 %all-to-all-done.1 = f32[32,2,8]{2,1,0:T(2,128)S(1)} async-done(((f32[32,2,8]{2,1,0:T(2,128)}), f32[32,2,8]{2,1,0:T(2,128)S(1)}, u32[]{:S(2)}, u32[]{:S(2)}) %all-to-all-start.1) | async-done | bytes 2080 | tf_op jit(solution)/shard_map/all_to_all | solution.py:9
  255.3 0.7 multiply_reduce_fusion
  256.0 1.2 fusion
  257.2 36.9 %all-gather.8.cloned.1.call-done = bf16[384,4096]{1,0:T(8,128)(2,1)} async-done(((bf16[384,512]{1,0:T(8,128)(2,1)}), bf16[384,4096]{1,0:T(8,128)(2,1)}) %all-gather.8.cloned.1.call-update) | async-done | bytes 3145744 | tf_op jit(solution)/shard_map/all_gather | solution.py:127
  294.2 8.8 %convolution_convert_fusion = bf16[4096,1024]{1,0:T(8,128)(2,1)} fusion(bf16[384,4096]{1,0:T(8,128)(2,1)} %all-gather.8.cloned.1.call-done, f32[384,1024]{1,0:T(8,128)S(1)} %fusion.20), kind=kOutput, calls=%fused_computation | convolution fusion | flops 3227385856 | bytes 13107200 | tf_op jit(solution)/shard_map/dot_general | solution.py:84
  303.0 1.3 broadcast_in_dim.52
  304.3 11.9 %all-to-all-start.2 = ((f32[32,1,1]{2,1,0:T(1,128)}), f32[32,1,1]{2,1,0:T(1,128)S(1)}, u32[]{:S(2)}, u32[]{:S(2)}) async-start(f32[32,1,1]{2,1,0:T(1,128)} %broadcast_in_dim.52), calls=%async_computation.3 | async-start | bytes 32768 | tf_op jit(solution)/shard_map/all_to_all | solution.py:9
  316.4 9.1 %all-to-all-done.2 = f32[32,1,1]{2,1,0:T(1,128)S(1)} async-done(((f32[32,1,1]{2,1,0:T(1,128)}), f32[32,1,1]{2,1,0:T(1,128)S(1)}, u32[]{:S(2)}, u32[]{:S(2)}) %all-to-all-start.2) | async-done | bytes 160 | tf_op jit(solution)/shard_map/all_to_all | solution.py:9
  325.5 0.9 broadcast_in_dim.53
  326.4 4.2 all-to-all-start.4
  330.6 10.0 %convolution_convert_fusion.2 = bf16[1024,512]{0,1:T(8,128)(2,1)} fusion(bf16[384,512]{1,0:T(8,128)(2,1)S(1)} %copy-done, f32[384,1024]{1,0:T(8,128)S(1)} %fusion.20, bf16[384,4096]{1,0:T(8,128)(2,1)} %all-gather.8.cloned.1.call-done, bf16[1024,4096]{1,0:T(8,128)(2,1)} %all-gather.6.cloned.1.call-done), kind=kOutput, calls=%fused_computation.6 | convolution fusion | flops 3627941888 | bytes 14548992 | tf_op jit(solution)/shard_map/dot_general | solution.py:84
  340.6 8.0 %all-to-all-done.4 = f32[32,512,8]{1,2,0:T(8,128)S(1)} async-done(((f32[32,512,8]{1,2,0:T(8,128)}), f32[32,512,8]{1,2,0:T(8,128)S(1)}, u32[]{:S(2)}, u32[]{:S(2)}) %all-to-all-start.4) | async-done | bytes 524320 | tf_op jit(solution)/shard_map/all_to_all | solution.py:9
  348.6 4.5 %all-to-all-start.3 = ((bf16[32,16,1024]{2,1,0:T(8,128)(2,1)}), bf16[32,16,1024]{2,1,0:T(8,128)(2,1)S(1)}, u32[]{:S(2)}, u32[]{:S(2)}) async-start(bf16[32,16,1024]{2,1,0:T(8,128)(2,1)} %bitcast.42), calls=%async_computation.4 | async-start | bytes 2097152 | tf_op jit(solution)/shard_map/all_to_all | solution.py:70
  353.1 0.6 reduce_sum.47
  354.4 0.7 reduce_sum.49
  355.1 28.9 %all-to-all-done.3 = bf16[32,16,1024]{2,1,0:T(8,128)(2,1)S(1)} async-done(((bf16[32,16,1024]{2,1,0:T(8,128)(2,1)}), bf16[32,16,1024]{2,1,0:T(8,128)(2,1)S(1)}, u32[]{:S(2)}, u32[]{:S(2)}) %all-to-all-start.3) | async-done | bytes 1048608 | tf_op jit(solution)/shard_map/all_to_all | solution.py:70
  384.0 0.8 convert_reduce_fusion
  384.8 55.6 %reduce-scatter.5.cloned.1.call-done = bf16[128,1024]{1,0:T(8,128)(2,1)} async-done(((bf16[4096,1024]{1,0:T(8,128)(2,1)}), bf16[128,1024]{1,0:T(8,128)(2,1)}) %reduce-scatter.5.cloned.1.call-update) | async-done | bytes 262160 | tf_op jit(solution)/shard_map/reduce_scatter | solution.py:139
  440.4 1.0 convert_bitcast_fusion
  441.4 1.0 copy.22
  (170 shorter events, 8.6 us)
Async XLA Ops:
  7.2 59.6 %copy-start = (bf16[384,512]{1,0:T(8,128)(2,1)S(1)}, bf16[384,512]{1,0:T(8,128)(2,1)}, u32[]{:S(2)}) copy-start(bf16[384,512]{1,0:T(8,128)(2,1)} %param.8) | copy-start | bytes 1179652
  7.2 59.6 %all-gather.4.cloned.1.call-start = ((), (), s32[]{:S(2)}) async-start(), calls=%async_computation.7 | async-start | bytes 1081344 | tf_op jit(solution)/shard_map/all_gather | solution.py:95
  7.9 143.3 %all-gather.6.cloned.1.call-start = ((), (), s32[]{:S(2)}) async-start(), calls=%async_computation.8 | async-start | bytes 8650752 | tf_op jit(solution)/shard_map/all_gather | solution.py:101
  8.7 193.9 %reduce-scatter.3.cloned.1.call-start = ((), (), s32[]{:S(2)}) async-start(), calls=%async_computation.9 | async-start | bytes 3538944 | tf_op jit(solution)/shard_map/reduce_scatter | solution.py:104
  159.4 0.7 copy-start.5
  159.4 5.0 %copy-start.6 = (f32[8]{0:T(128)S(1)}, f32[8]{0:T(128)}, u32[]{:S(2)}) copy-start(f32[8]{0:T(128)} %param.13) | copy-start | bytes 100
  159.4 5.0 %copy-start.7 = (f32[8]{0:T(128)S(1)}, f32[8]{0:T(128)}, u32[]{:S(2)}) copy-start(f32[8]{0:T(128)} %param.14) | copy-start | bytes 100
  159.4 44.4 %copy-start.4 = (bf16[512,8]{0,1:T(8,128)(2,1)S(1)}, bf16[512,8]{0,1:T(8,128)(2,1)}, u32[]{:S(2)}) copy-start(bf16[512,8]{0,1:T(8,128)(2,1)} %param.11) | copy-start | bytes 24580
  160.1 64.5 %copy-start.3 = (f32[8,384]{1,0:T(8,128)S(1)}, f32[8,384]{1,0:T(8,128)}, u32[]{:S(2)}) copy-start(f32[8,384]{1,0:T(8,128)} %param.12) | copy-start | bytes 36868
  161.3 47.3 %collective-permute-start = (s32[1]{0:T(128)}, s32[1]{0:T(128)}, u32[]{:S(2)}, u32[]{:S(2)}) collective-permute-start(s32[1]{0:T(128)} %add.218), channel_id=1, source_target_pairs={{8,0},{16,8},{24,16},{32,24},{40,32},{48,40},{56,48},{64,56},{72,6... | collective-permute-start | bytes 20 | tf_op jit(solution)/shard_map/ppermute | solution.py:21
  204.0 51.9 %copy-start.1 = (bf16[384,512]{1,0:T(8,128)(2,1)S(1)}, bf16[384,512]{1,0:T(8,128)(2,1)}, u32[]{:S(2)}) copy-start(bf16[384,512]{1,0:T(8,128)(2,1)} %reduce-scatter.3.cloned.1.call-done) | copy-start | bytes 1179652
  204.7 9.2 %all-to-all-start = ((f32[8,384,8]{1,2,0:T(8,128)}), f32[8,384,8]{1,2,0:T(8,128)S(1)}, u32[]{:S(2)}, u32[]{:S(2)}) async-start(f32[8,384,8]{1,2,0:T(8,128)} %broadcast_in_dim.26), calls=%async_computation.1 | async-start | bytes 196608 | tf_op jit(solution)/shard_map/all_to_all | solution.py:9
  214.0 10.7 %collective-permute-start.1 = (f32[8,1]{1,0:T(8,128)S(1)}, f32[8,1]{1,0:T(8,128)S(1)}, u32[]{:S(2)}, u32[]{:S(2)}) collective-permute-start(f32[8,1]{1,0:T(8,128)S(1)} %slice.468), channel_id=1, source_target_pairs={{8,0},{16,8},{24,16},{32,24},{40,32},{48,40},{56,48},{64,56},{72,6... | collective-permute-start | bytes 104 | tf_op jit(solution)/shard_map/ppermute | solution.py:21
  238.0 16.8 %all-to-all-start.1 = ((f32[32,2,8]{2,1,0:T(2,128)}), f32[32,2,8]{2,1,0:T(2,128)S(1)}, u32[]{:S(2)}, u32[]{:S(2)}) async-start(f32[32,2,8]{2,1,0:T(2,128)} %broadcast_in_dim.28), calls=%async_computation.2 | async-start | bytes 65536 | tf_op jit(solution)/shard_map/all_to_all | solution.py:9
  245.1 49.0 %all-gather.8.cloned.1.call-start = ((), (), s32[]{:S(2)}) async-start(), calls=%async_computation.10 | async-start | bytes 3538944 | tf_op jit(solution)/shard_map/all_gather | solution.py:127
  256.0 60.3 %copy-start.2 = (f32[8,384]{1,0:T(8,128)}, f32[8,384]{1,0:T(8,128)S(1)}, u32[]{:S(2)}) copy-start(f32[8,384]{1,0:T(8,128)S(1)} %get-tuple-element.26) | copy-start | bytes 36868
  257.2 183.2 %reduce-scatter.5.cloned.1.call-start = ((), (), s32[]{:S(2)}) async-start(), calls=%async_computation.11 | async-start | bytes 8650752 | tf_op jit(solution)/shard_map/reduce_scatter | solution.py:139
  304.3 21.2 %all-to-all-start.2 = ((f32[32,1,1]{2,1,0:T(1,128)}), f32[32,1,1]{2,1,0:T(1,128)S(1)}, u32[]{:S(2)}, u32[]{:S(2)}) async-start(f32[32,1,1]{2,1,0:T(1,128)} %broadcast_in_dim.52), calls=%async_computation.3 | async-start | bytes 32768 | tf_op jit(solution)/shard_map/all_to_all | solution.py:9
  326.4 22.2 %all-to-all-start.4 = ((f32[32,512,8]{1,2,0:T(8,128)}), f32[32,512,8]{1,2,0:T(8,128)S(1)}, u32[]{:S(2)}, u32[]{:S(2)}) async-start(f32[32,512,8]{1,2,0:T(8,128)} %broadcast_in_dim.53), calls=%async_computation.6 | async-start | bytes 1048576 | tf_op jit(solution)/shard_map/all_to_all | solution.py:9
  348.6 35.4 %all-to-all-start.3 = ((bf16[32,16,1024]{2,1,0:T(8,128)(2,1)}), bf16[32,16,1024]{2,1,0:T(8,128)(2,1)S(1)}, u32[]{:S(2)}, u32[]{:S(2)}) async-start(bf16[32,16,1024]{2,1,0:T(8,128)(2,1)} %bitcast.42), calls=%async_computation.4 | async-start | bytes 2097152 | tf_op jit(solution)/shard_map/all_to_all | solution.py:70
Sparse Core Ops, SparseCore 0:
  10.5 56.1 all-gather.3
  69.2 81.9 all-gather.5
  159.6 42.9 reduce-scatter.2
  257.3 36.8 all-gather.7
  303.2 137.1 reduce-scatter.4
where the time goes:
time: 451 us; the launch traced here: 450 us
  waiting for transfers between devices  336 us (75%)
  starting transfers between devices  42.3 us (9%)
  matrix products  30.4 us (7%)
  between operations  16.8 us (4%)
  local copies, waits for them, and re-layouts  16.5 us (4%)
  other arithmetic  8.07 us (2%)
    all_gather x1, waiting for transfers between devices, shards(): lax.all_gather(w_second, 'batch', axis=1, tiled=True)  82.7 us
    all_gather x1, waiting for transfers between devices, shards(): lax.all_gather(w_first, 'batch', axis=0, tiled=True)  58 us
    reduce_scatter x1, waiting for transfers between devices, shards(): lax.psum_scatter(contract(columns, hidden_first, 0, 0).astype(jnp.bfloat1...  55.6 us
    reduce_scatter x1, waiting for transfers between devices, shards(): lax.psum_scatter(partial_value.astype(jnp.bfloat16), 'hidden', scatter_di...  38.1 us
    all_gather x1, waiting for transfers between devices, shards(): slope_second = lax.all_gather(slope_share, 'hidden', axis=1, tiled=True)  36.9 us
    all_to_all x4, waiting for transfers between devices, sent_to_all(): lax.all_to_all(jnp.broadcast_to(array[None], (length, *array.shape)), axi...  30.9 us
    all_to_all x1, waiting for transfers between devices, summed_on_arrival(): lax.all_to_all(cut_along(array, dim, length), axis, 0, 0, tiled=True)  28.9 us
    all_to_all x4, starting transfers between devices, sent_to_all(): lax.all_to_all(jnp.broadcast_to(array[None], (length, *array.shape)), axi...  27.1 us
  transfers between devices with their start and end apart: 12, of which 11 were waited for; matrix products, arithmetic and copies ran while one was open for 4% of the time, Pallas kernels for 0%

commit v1 on v0

v1 whole, which is shorter than its diff:
```python
import functools

import jax
import jax.numpy as jnp
from jax import lax
from jax.experimental import pallas as pl
from jax.experimental.pallas import tpu as pltpu
from jax.sharding import PartitionSpec as P

BF16, F32 = jnp.bfloat16, jnp.float32
MESH = pl.DeviceIdType.MESH
SLOTS = 240
LOW, HIGH = pl.ds(0, 512), pl.ds(512, 512)


def dot(left, right, dims=((1,), (0,))):
    return lax.dot_general(left, right, (dims, ((), ())), preferred_element_type=F32)


def mod(value, count):
    return lax.rem(value + count, count)


def lane(dx):
    return pl.ds(dx * 128, 128)


class Links:
    def __init__(self, sent, came):
        self.sent, self.came, self.used, self.open = sent, came, 0, []

    def take(self):
        self.used += 1
        return self.used - 1

    def make(self, src, dst, to, k, k_came=None):
        return pltpu.make_async_remote_copy(
            src_ref=src,
            dst_ref=dst,
            send_sem=self.sent.at[k],
            recv_sem=self.came.at[k if k_came is None else k_came],
            device_id=to,
            device_id_type=MESH,
        )

    def push(self, src, dst, to, land=None):
        k = self.take()
        copy = self.make(src, dst, to, k)
        copy.start()
        self.open.append(copy)
        return copy if land is None else self.make(land, land, to, k)

    def drain(self):
        for copy in self.open:
            copy.wait_send()
        self.open = []


def kernel(
    feat, w1in, w2in, whin, rein, dt,
    adv_o, loss_o, g1_o, g2_o, gh_o,
    F, FT, W1, W2, WHB, WH, RE, HF, HFT, SP, PS, RA, RB, RL, RR, RZ, PRE, SL2, H2,
    V, ADV, S, BACK, G2, XA, XB, XL, XR, ZA, ZB, ZL, ZR, BKS, BKR, SF,
    G1, YA, YB, YL, YR, UA, UB, UL, UR, GF, GT, GHP, GR, GS, GZ, GX, GY, GC, GH,
    sent, came,
):
    b, j = lax.axis_index("batch"), lax.axis_index("hidden")
    c, m = lax.rem(b, 2), lax.div(b, 2)
    zh, x = lax.rem(m, 4), lax.div(m, 4)
    y, zl = lax.rem(j, 4), lax.div(j, 4)
    r = y * 2 + zl
    link = Links(sent, came)
    push = link.push

    def at(dx=0, dz=0, dc=0, dy=0, dl=0):
        bb = (mod(x + dx, 4) * 4 + mod(zh + dz, 4)) * 2 + mod(c + dc, 2)
        return bb, mod(zl + dl, 2) * 4 + mod(y + dy, 4)

    def beside(step, dc, dy, dl):
        bb = mod(m + step, 16) * 2 + mod(c + dc, 2)
        return bb, mod(zl + dl, 2) * 4 + mod(y + dy, 4)

    peers = [(dc, dy, dl) for dc in range(2) for dy in range(4) for dl in range(2)]

    F[c] = feat[...]
    W1[x, zh, c] = w1in[...]
    W2[0, :, lane(0)] = w2in[...]
    WHB[j] = whin[...]
    RE[c] = rein[...]

    barrier = pltpu.get_barrier_semaphore()
    partners = [at(dc=dc, dy=dy, dl=dl) for dc, dy, dl in peers[1:]]
    partners += [at(dx=d) for d in (1, 2, 3)] + [at(dz=d) for d in (1, 2, 3)]
    partners += [beside(step, *peer) for step in (1, -1) for peer in peers]
    for partner in partners:
        pl.semaphore_signal(barrier, inc=1, device_id=partner, device_id_type=MESH)
    pl.semaphore_wait(barrier, len(partners))

    w1z = {
        dz: push(w1in, W1.at[x, zh, c], at(dz=dz), W1.at[x, mod(zh - dz, 4), c])
        for dz in (1, 3, 2)
    }

    def w1_sides(zs):
        own = W1.at[x, zs, c]
        return [
            push(own, own, at(dx=dx), W1.at[mod(x - dx, 4), zs, c]) for dx in (1, 3)
        ]

    def w1_across(zs, sides):
        out = []
        for dx, half, side in ((1, LOW, sides[0]), (3, HIGH, sides[1])):
            side.wait_recv()
            part = W1.at[mod(x - dx, 4), zs, c, :, half]
            out.append(push(part, part, at(dx=dx), W1.at[mod(x + 2, 4), zs, c, :, half]))
        return out

    w1x = {0: w1_sides(zh)}
    feat_in = push(feat, F.at[c], at(dc=1), F.at[1 - c])
    first = [
        push(w2in.at[LOW], W2.at[3, LOW, lane(0)], at(dz=1)),
        push(w2in.at[HIGH], W2.at[1, HIGH, lane(0)], at(dz=3)),
    ]
    w2x = {}

    def w2_side(dz, half):
        src = W2.at[dz, half, lane(0)]
        right = lambda: push(src, W2.at[dz, half, lane(3)], at(dx=1))
        left = lambda: push(src, W2.at[dz, half, lane(1)], at(dx=3))
        if half is LOW:
            w2x[dz, 3, 0] = right()
            w2x[dz, 1, 0] = left()
        else:
            w2x[dz, 1, 1] = left()
            w2x[dz, 3, 1] = right()

    def w2_across(dz):
        w2x[dz, 3, 0].wait_recv()
        w2x[dz, 2, 0] = push(
            W2.at[dz, LOW, lane(3)], W2.at[dz, LOW, lane(2)], at(dx=1)
        )
        w2x[dz, 1, 1].wait_recv()
        w2x[dz, 2, 1] = push(
            W2.at[dz, HIGH, lane(1)], W2.at[dz, HIGH, lane(2)], at(dx=3)
        )

    def w2_rest(dz):
        for key in ((3, 1), (1, 0), (2, 0), (2, 1)):
            w2x[(dz, *key)].wait_recv()

    second = [
        push(w2in.at[HIGH], W2.at[3, HIGH, lane(0)], at(dz=1)),
        push(w2in.at[LOW], W2.at[1, LOW, lane(0)], at(dz=3)),
    ]
    for dz in (1, 3, 2):
        w1z[dz].wait_recv()
        w1x[dz] = w1_sides(mod(zh - dz, 4))
    w2_side(0, LOW)
    w2_side(0, HIGH)
    re_in = push(rein, RE.at[c], at(dc=1), RE.at[1 - c])
    re_sem = [link.take() for _ in range(2)]
    re_to = [
        link.make(rein, RE.at[2], beside(-1, dc, 0, 0), re_sem[dc], re_sem[0])
        for dc in range(2)
    ]

    @pl.when(c == 0)
    def _():
        for copy in re_to:
            copy.start()

    wh_in = [
        push(whin, WHB.at[j], at(dy=dy, dl=dl), WHB.at[mod(zl - dl, 2) * 4 + mod(y - dy, 4)])
        for dc, dy, dl in peers[1:8]
    ]

    w1far = {0: w1_across(zh, w1x[0])}
    for dz in (1, 3, 2):
        w1far[dz] = w1_across(mod(zh - dz, 4), w1x[dz])
    w2_across(0)
    w1core = []
    for dz in (0, 1, 3, 2):
        for copy in w1far[dz]:
            copy.wait_recv()
        zs = mod(zh - dz, 4)
        w1core.append(
            push(W1.at[:, zs, c], W1.at[:, zs, c], at(dc=1), W1.at[:, zs, 1 - c])
        )
    first[0].wait_recv()
    w2_z2 = [push(W2.at[3, LOW, lane(0)], W2.at[2, LOW, lane(0)], at(dz=1))]
    w2_side(3, LOW)
    first[1].wait_recv()
    w2_z2.append(push(W2.at[1, HIGH, lane(0)], W2.at[2, HIGH, lane(0)], at(dz=3)))
    w2_side(1, HIGH)

    feat_in.wait_recv()
    for copy in w1core:
        copy.wait_recv()

    @pl.loop(0, 4)
    def _(n):
        cols = pl.ds(pl.multiple_of(n * 256, 256), 256)
        weights = W1[:, :, :, :, cols].reshape(512, 256)
        SP[:, cols] = dot(F[...].reshape(768, 512), weights)

        @pl.loop(0, 12)
        def _(i):
            rows = pl.ds(pl.multiple_of(i * 64, 64), 64)
            value = SP[rows, cols]
            gate = 1.0 / (1.0 + jnp.exp(-value))
            HF[rows, cols] = (value * gate).astype(BF16)
            SP[rows, cols] = gate * (1.0 + value * (1.0 - gate))

    def product(dz):
        @pl.loop(0, 2)
        def _(n):
            start = pl.multiple_of(n * 256, 256)
            part = dot(HF[...], W2[dz, :, pl.ds(start, 256)])
            into = pl.ds(pl.multiple_of(dz * 512 + n * 256, 256), 256)
            PS[:, :, into] = part.astype(BF16).reshape(8, 96, 256)

    up, down, over = mod(y + 1, 4), mod(y - 1, 4), mod(y + 2, 4)
    came_rs = {}

    def scatter_a(dz):
        at_dz = pl.ds(dz * 512, 512)
        came_rs[dz] = [
            push(PS.at[over * 2, :, at_dz], RA.at[dz], at(dy=1)),
            push(PS.at[over * 2 + 1, :, at_dz], RB.at[dz], at(dy=3)),
            push(PS.at[up * 2 + 1, :, at_dz], RL.at[dz, 1], at(dy=1)),
            push(PS.at[down * 2, :, at_dz], RR.at[dz, 0], at(dy=3)),
        ]

    def scatter_b(dz):
        at_dz = pl.ds(dz * 512, 512)
        for got, buf, row, dst, dy in (
            (came_rs[dz][0], RA, up * 2, RL.at[dz, 0], 1),
            (came_rs[dz][1], RB, down * 2 + 1, RR.at[dz, 1], 3),
        ):
            got.wait_recv()
            total = PS[row, :, at_dz].astype(F32) + buf[dz].astype(F32)
            PS[row, :, at_dz] = total.astype(BF16)
            came_rs[dz].append(push(PS.at[row, :, at_dz], dst, at(dy=dy)))

    def scatter_c(dz):
        at_dz = pl.ds(dz * 512, 512)
        for got in came_rs[dz][2:]:
            got.wait_recv()

        def total(side):
            return (
                PS[y * 2 + side, :, at_dz].astype(F32)
                + RL[dz, side].astype(F32)
                + RR[dz, side].astype(F32)
            )

        PS[y * 2 + 1 - zl, :, at_dz] = total(1 - zl).astype(BF16)
        came_rs[dz].append(
            push(PS.at[y * 2 + 1 - zl, :, at_dz], RZ.at[dz], at(dl=1))
        )
        PRE[:, at_dz] = total(zl)

    def scatter_d(dz):
        at_dz = pl.ds(dz * 512, 512)
        came_rs[dz][-1].wait_recv()

        @pl.loop(0, 3)
        def _(i):
            rows = pl.ds(pl.multiple_of(i * 32, 32), 32)
            value = PRE[rows, at_dz] + RZ[dz, rows, :].astype(F32)
            gate = 1.0 / (1.0 + jnp.exp(-value))
            H2[rows, at_dz] = (value * gate).astype(BF16)
            SL2[rows, at_dz] = gate * (1.0 + value * (1.0 - gate))

    w2_rest(0)
    product(0)
    scatter_a(0)
    second[0].wait_recv()
    w2_side(3, HIGH)
    second[1].wait_recv()
    w2_side(1, LOW)
    w2_across(3)
    w2_across(1)
    scatter_b(0)
    w2_z2[0].wait_recv()
    w2_side(2, LOW)
    w2_z2[1].wait_recv()
    w2_side(2, HIGH)

    @pl.loop(0, 4)
    def _(n):
        cols = pl.ds(pl.multiple_of(n * 256, 256), 256)
        HFT[cols, :] = HF[:, cols].astype(F32).T.astype(BF16)

    w2_rest(3)
    product(3)
    scatter_a(3)
    scatter_c(0)

    @pl.loop(0, 2)
    def _(n):
        cols = pl.ds(pl.multiple_of(n * 256, 256), 256)
        FT[cols, :] = F[:, :, cols].reshape(768, 256).astype(F32).T.astype(BF16)

    for copy in wh_in:
        copy.wait_recv()
    for dz in range(4):
        for dx in range(4):
            mm = mod(x + dx, 4) * 4 + mod(zh + dz, 4)
            group, pair = lax.div(mm, 2), lax.rem(mm, 2)
            even, odd = (
                jnp.where(c == 0, WHB[group, :, lane(2 * p)], WHB[group, :, lane(2 * p + 1)])
                for p in (0, 1)
            )
            WH[:, lane(dz * 4 + dx)] = jnp.where(pair == 0, even, odd).astype(BF16)

    scatter_b(3)
    w2_rest(1)
    product(1)
    scatter_a(1)
    w2_across(2)
    scatter_d(0)
    scatter_c(3)
    scatter_b(1)
    scatter_d(3)
    scatter_c(1)
    w2_rest(2)
    product(2)
    scatter_a(2)
    scatter_d(1)
    scatter_b(2)
    scatter_c(2)
    scatter_d(2)

    wide = jnp.zeros((8, 32), F32)
    own_values = dot(WH[...], H2[...], ((1,), (1,)))
    V[c, r] = jnp.concatenate([own_values, wide], axis=1)
    v_in = []
    for dc, dy, dl in peers[1:]:
        src_r = mod(y - dy, 4) * 2 + mod(zl - dl, 2)
        v_in.append(
            push(V.at[c, r], V.at[c, r], at(dc=dc, dy=dy, dl=dl), V.at[mod(c - dc, 2), src_r])
        )
    v_out, v_next = [], []
    for dc, dy, dl in peers:
        k = link.take()
        src_r = mod(y - dy, 4) * 2 + mod(zl - dl, 2)
        v_out.append(
            link.make(V.at[c, r], V.at[c, 8 + lax.rem(r, 4)], beside(-1, dc, dy, dl), k)
        )
        land = V.at[mod(c - dc, 2), 8 + lax.rem(src_r, 4)]
        v_next.append((src_r, link.make(land, land, beside(-1, dc, dy, dl), k)))

    @pl.when(r < 4)
    def _():
        for copy in v_out:
            copy.start()

    re_in.wait_recv()
    link.make(RE.at[2], RE.at[2], at(dc=1), re_sem[0], re_sem[0]).wait_recv()
    shape = (8, 12 * 128)
    place = lax.rem(lax.broadcasted_iota(jnp.int32, shape, 1), 128)

    def ahead(array, steps):
        return pltpu.roll(array, shape[1] - steps, 1)

    def following(array):
        return jnp.where(place == 95, ahead(array, 33), ahead(array, 1))

    def row_of(kind):
        return jnp.concatenate([RE[i // 4, kind, i % 4] for i in range(12)], axis=1)

    reward, number = row_of(0), row_of(1)
    discount = jnp.concatenate([dt[0]] * 12, axis=1)
    both = jnp.concatenate([dt[0] * dt[1]] * 12, axis=1)
    keep = jnp.where(following(number) == number, 1.0, 0.0)
    real = place < 96
    factor = jnp.where(real, both * keep, 1.0)
    scale = discount * keep

    for copy in v_in:
        copy.wait_recv()
    for src_r, copy in v_next:

        @pl.when(src_r < 4)
        def _():
            copy.wait_recv()

    value = jnp.concatenate([V[0, i] + V[1, i] for i in range(12)], axis=1)
    total = jnp.where(real, reward + scale * following(value) - value, 0.0)
    step = 1
    while step < shape[1]:
        total = total + factor * ahead(total, step)
        factor = factor * ahead(factor, step)
        step *= 2
    for i in range(12):
        ADV[i] = total[:, i * 128 : (i + 1) * 128]

    own = ADV[r]
    slope_t = (-own[:, :96]).astype(BF16)
    slope = (-own).T[:96, :].astype(BF16)
    own_rows = S.at[r]

    def slope_chunk(dz):
        at_dz = pl.ds(dz * 512, 512)
        own_rows[:, at_dz] = (dot(slope, WH[:, at_dz]) * SL2[:, at_dz]).astype(BF16)

    ag = {}
    pair_r = y * 2 + 1 - zl

    def gather_a(dz):
        at_dz = pl.ds(dz * 512, 512)
        src = S.at[r, :, at_dz]
        ag[dz] = {
            "pair": push(src, src, at(dl=1), S.at[pair_r, :, at_dz]),
            "down": push(src, src, at(dy=1), S.at[down * 2 + zl, :, at_dz]),
            "up": push(src, src, at(dy=3), S.at[up * 2 + zl, :, at_dz]),
        }

    def gather_b(dz):
        at_dz = pl.ds(dz * 512, 512)
        ag[dz]["pair"].wait_recv()
        src = S.at[pair_r, :, at_dz]
        ag[dz]["down2"] = push(src, src, at(dy=1), S.at[down * 2 + 1 - zl, :, at_dz])
        ag[dz]["up2"] = push(src, src, at(dy=3), S.at[up * 2 + 1 - zl, :, at_dz])

    def gather_c(dz):
        at_dz = pl.ds(dz * 512, 512)
        for name in ("down", "up", "down2", "up2"):
            ag[dz][name].wait_recv()
        low, high = S.at[down * 2, :, at_dz], S.at[up * 2 + 1, :, at_dz]
        ag[dz]["far"] = [
            push(low, low, at(dy=1), S.at[over * 2, :, at_dz]),
            push(high, high, at(dy=3), S.at[over * 2 + 1, :, at_dz]),
        ]

    def gather_d(dz):
        for got in ag[dz]["far"]:
            got.wait_recv()

    def grad_second(dz):
        at_dz = pl.ds(dz * 512, 512)

        @pl.loop(0, 4)
        def _(n):
            rows = pl.ds(pl.multiple_of(n * 256, 256), 256)
            G2[dz, rows, :] = dot(HFT[rows, :], S[:, :, at_dz].reshape(768, 512)).astype(BF16)

    def back_first(dz, start):
        at_dz = pl.ds(dz * 512, 512)

        @pl.loop(0, 4)
        def _(n):
            cols = pl.ds(pl.multiple_of(n * 256, 256), 256)
            part = dot(S[:, :, at_dz].reshape(768, 512), W2[dz, cols, :], ((1,), (1,)))
            BACK[:, cols] = part if start else BACK[:, cols] + part

    gx = {}

    def reduce_a(dz):
        gx[dz] = [
            push(G2.at[dz, LOW, lane(2)], XA.at[dz], at(dx=1)),
            push(G2.at[dz, HIGH, lane(2)], XB.at[dz], at(dx=3)),
            push(G2.at[dz, HIGH, lane(1)], XL.at[dz, 1], at(dx=1)),
            push(G2.at[dz, LOW, lane(3)], XR.at[dz, 0], at(dx=3)),
        ]

    def reduce_b(dz):
        for got, buf, half, dx, dst in (
            (gx[dz][0], XA, LOW, 1, XL.at[dz, 0]),
            (gx[dz][1], XB, HIGH, 3, XR.at[dz, 1]),
        ):
            got.wait_recv()
            block = G2[dz, half, lane(dx)].astype(F32) + buf[dz].astype(F32)
            G2[dz, half, lane(dx)] = block.astype(BF16)
            gx[dz].append(push(G2.at[dz, half, lane(dx)], dst, at(dx=dx)))

    def reduce_c(dz, into=None):
        for got in gx[dz][2:]:
            got.wait_recv()
        for side, half in ((0, LOW), (1, HIGH)):
            block = (
                G2[dz, half, lane(0)].astype(F32)
                + XL[dz, side].astype(F32)
                + XR[dz, side].astype(F32)
            )
            if into is None:
                G2[dz, half, lane(0)] = block.astype(BF16)
            else:
                into[half, :] = block

    slope_chunk(2)
    gather_a(2)
    slope_chunk(1)
    gather_a(1)
    slope_chunk(3)
    slope_chunk(0)
    gather_b(2)

    for i in range(4):
        adv_o[i] = ADV[4 * c + i]
    small = lax.broadcasted_iota(jnp.int32, (8, 128), 1) < 96
    own_loss = jnp.where(small, own * own, 0.0)
    head = dot(slope_t, H2[...])
    for dz in range(4):
        for dx in range(4):
            mm = mod(x + dx, 4) * 4 + mod(zh + dz, 4)
            GHP[lax.div(mm, 2), lax.rem(mm, 2)] = head[:, (dz * 4 + dx) * 128 :][:, :128]
    for g in range(8):
        GHP[g, 2] = own_loss
    gather_c(2)
    gh_in = []
    for dc, dy, dl in peers[1:8]:
        to_j = mod(zl + dl, 2) * 4 + mod(y + dy, 4)
        from_j = mod(zl - dl, 2) * 4 + mod(y - dy, 4)
        gh_in.append(push(GHP.at[to_j], GR.at[j], at(dy=dy, dl=dl), GR.at[from_j]))
    GR[j] = GHP[j]
    gather_b(1)
    gather_a(3)
    gather_d(2)
    grad_second(2)
    reduce_a(2)
    gather_c(1)
    gather_b(3)
    back_first(2, True)
    gather_a(0)
    reduce_b(2)
    gather_d(1)
    grad_second(1)
    reduce_a(1)
    gather_c(3)
    gather_b(0)
    back_first(1, False)
    reduce_b(1)
    for got in gh_in:
        got.wait_recv()
    GS[...] = functools.reduce(jnp.add, [GR[i] for i in range(8)])
    gz_in = [push(GS, GZ.at[d - 1], at(dz=d)) for d in (1, 2, 3)]
    gather_d(3)
    grad_second(3)
    reduce_a(3)
    gather_c(0)
    reduce_c(2)
    z_in = [
        push(G2.at[2, LOW, lane(0)], ZA, at(dz=1)),
        push(G2.at[2, HIGH, lane(0)], ZB, at(dz=3)),
    ]
    back_first(3, False)
    reduce_b(3)
    gather_d(0)
    back_first(0, False)

    @pl.loop(0, 12)
    def _(i):
        rows = pl.ds(pl.multiple_of(i * 64, 64), 64)
        other = pl.ds(pl.multiple_of((1 - c) * 512, 512), 512)
        BKS[rows, :] = BACK[rows, other].astype(BF16)

    back_in = push(BKS, BKR, at(dc=1))
    grad_second(0)
    reduce_a(0)
    for got in gz_in:
        got.wait_recv()
    GY[...] = GS[...] + GZ[0] + GZ[1] + GZ[2]
    gxs_in = [push(GY, GX.at[d - 1], at(dx=d)) for d in (1, 2, 3)]
    back_in.wait_recv()

    @pl.loop(0, 12)
    def _(i):
        rows = pl.ds(pl.multiple_of(i * 64, 64), 64)
        mine = pl.ds(pl.multiple_of(c * 512, 512), 512)
        back = BACK[rows, mine] + BKR[rows, :].astype(F32)
        SF[rows, :] = (back * SP[rows, mine]).astype(BF16)

    @pl.loop(0, 2)
    def _(n):
        rows = pl.ds(pl.multiple_of(n * 256, 256), 256)
        part = dot(FT[rows, :], SF[...]).astype(BF16)
        G1[pl.ds(2 * n, 2)] = part.reshape(2, 4, 32, 512)

    lo, hi = pl.ds(0, 16), pl.ds(16, 16)
    x1, x3, x2 = mod(x + 1, 4), mod(x - 1, 4), mod(x + 2, 4)
    z1, z3, z2 = mod(zh + 1, 4), mod(zh - 1, 4), mod(zh + 2, 4)
    yin = [
        push(G1.at[x2, :, lo], YA, at(dx=1)),
        push(G1.at[x2, :, hi], YB, at(dx=3)),
        push(G1.at[x1, :, hi], YL.at[1], at(dx=1)),
        push(G1.at[x3, :, lo], YR.at[0], at(dx=3)),
    ]
    reduce_c(1)
    reduce_c(3)
    z_in += [
        push(G2.at[1, HIGH, lane(0)], ZL.at[1], at(dz=1)),
        push(G2.at[3, LOW, lane(0)], ZR.at[0], at(dz=3)),
    ]
    for got, buf, dz, half, dst in (
        (z_in[0], ZA, 1, LOW, ZL.at[0]),
        (z_in[1], ZB, 3, HIGH, ZR.at[1]),
    ):
        got.wait_recv()
        block = G2[dz, half, lane(0)].astype(F32) + buf[...].astype(F32)
        G2[dz, half, lane(0)] = block.astype(BF16)
        z_in.append(push(G2.at[dz, half, lane(0)], dst, at(dz=dz)))
    reduce_b(0)
    for got, buf, row, half, dst, dx in (
        (yin[0], YA, x1, lo, YL.at[0], 1),
        (yin[1], YB, x3, hi, YR.at[1], 3),
    ):
        got.wait_recv()
        block = G1[row, :, half].astype(F32) + buf[...].astype(F32)
        G1[row, :, half] = block.astype(BF16)
        yin.append(push(G1.at[row, :, half], dst, at(dx=dx)))
    for got in gxs_in:
        got.wait_recv()
    heads = GY[...] + GX[0] + GX[1] + GX[2]
    GH[...] = heads
    gc_in = push(GH, GC, at(dc=1))
    for got in yin[2:]:
        got.wait_recv()
    for side, half in ((0, lo), (1, hi)):
        block = G1[x, :, half].astype(F32) + YL[side].astype(F32) + YR[side].astype(F32)
        G1[x, :, half] = block.astype(BF16)
    uin = [
        push(G1.at[x, z2, lo], UA, at(dz=1)),
        push(G1.at[x, z2, hi], UB, at(dz=3)),
        push(G1.at[x, z1, hi], UL.at[1], at(dz=1)),
        push(G1.at[x, z3, lo], UR.at[0], at(dz=3)),
    ]
    gc_in.wait_recv()
    other = GC[...]
    loss_o[...] = jnp.broadcast_to(jnp.sum(heads[2]), (8, 128))
    for i in range(2):
        gh_o[:, lane(2 * i)] = jnp.where(c == 0, heads[i], other[i])
        gh_o[:, lane(2 * i + 1)] = jnp.where(c == 0, other[i], heads[i])
    for got, buf, row, half, dst, dz in (
        (uin[0], UA, z1, lo, UL.at[0], 1),
        (uin[1], UB, z3, hi, UR.at[1], 3),
    ):
        got.wait_recv()
        block = G1[x, row, half].astype(F32) + buf[...].astype(F32)
        G1[x, row, half] = block.astype(BF16)
        uin.append(push(G1.at[x, row, half], dst, at(dz=dz)))
    reduce_c(0, g2_o)
    for got in uin[2:]:
        got.wait_recv()
    for side, half in ((0, lo), (1, hi)):
        GF[side] = (
            G1[x, zh, half].astype(F32) + UL[side].astype(F32) + UR[side].astype(F32)
        )
    gt_in = push(GF.at[1 - c], GT, at(dc=1))
    for got in z_in[2:]:
        got.wait_recv()
    for side, half in ((0, LOW), (1, HIGH)):
        g2_o[half, :] = g2_o[half, :] + ZL[side].astype(F32) + ZR[side].astype(F32)
    gt_in.wait_recv()
    mine, theirs = GF[c], GT[...]
    g1_o[:, LOW] = jnp.where(c == 0, mine, theirs)
    g1_o[:, HIGH] = jnp.where(c == 0, theirs, mine)

    link.drain()

    @pl.when(c == 0)
    def _():
        for copy in re_to:
            copy.wait_send()

    @pl.when(r < 4)
    def _():
        for copy in v_out:
            copy.wait_send()


SCRATCH = [
    ((2, 384, 512), BF16), ((512, 768), BF16), ((4, 4, 2, 16, 1024), BF16),
    ((4, 1024, 512), BF16), ((8, 8, 512), F32), ((8, 2048), BF16), ((3, 2, 4, 8, 128), F32),
    ((768, 1024), BF16), ((1024, 768), BF16), ((768, 1024), F32), ((8, 96, 2048), BF16),
    ((4, 96, 512), BF16), ((4, 96, 512), BF16), ((4, 2, 96, 512), BF16),
    ((4, 2, 96, 512), BF16), ((4, 96, 512), BF16), ((96, 2048), F32), ((96, 2048), F32),
    ((96, 2048), BF16), ((2, 12, 8, 128), F32), ((12, 8, 128), F32), ((8, 96, 2048), BF16),
    ((768, 1024), F32), ((4, 1024, 512), BF16), ((4, 512, 128), BF16), ((4, 512, 128), BF16),
    ((4, 2, 512, 128), BF16), ((4, 2, 512, 128), BF16), ((512, 128), BF16),
    ((512, 128), BF16), ((2, 512, 128), BF16), ((2, 512, 128), BF16), ((768, 512), BF16),
    ((768, 512), BF16), ((768, 512), BF16), ((4, 4, 32, 512), BF16), ((4, 16, 512), BF16),
    ((4, 16, 512), BF16), ((2, 4, 16, 512), BF16), ((2, 4, 16, 512), BF16), ((16, 512), BF16),
    ((16, 512), BF16), ((2, 16, 512), BF16), ((2, 16, 512), BF16), ((2, 16, 512), F32),
    ((16, 512), F32), ((8, 3, 8, 128), F32), ((8, 3, 8, 128), F32), ((3, 8, 128), F32),
    ((3, 3, 8, 128), F32), ((3, 3, 8, 128), F32), ((3, 8, 128), F32), ((3, 8, 128), F32),
    ((3, 8, 128), F32),
]


def shards(features, w_first, w_second, w_head, rewards, discount, trace, episode):
    pad = ((0, 0), (0, 0), (0, 32))
    pieces = jnp.pad(rewards.reshape(8, 4, 96), pad).transpose(1, 0, 2)
    numbers = jnp.pad(episode.astype(F32).reshape(1, 4, 96), pad).transpose(1, 0, 2)
    rein = jnp.stack([pieces, jnp.broadcast_to(numbers, pieces.shape)])
    rates = jnp.broadcast_to(jnp.stack([discount, trace])[:, :, None], (2, 8, 128))
    heads = w_head.T.astype(F32)
    vmem = pl.BlockSpec(memory_space=pltpu.VMEM)
    advantages, loss, grad_first, grad_second, grad_head = pl.pallas_call(
        kernel,
        out_shape=(
            jax.ShapeDtypeStruct((4, 8, 128), F32),
            jax.ShapeDtypeStruct((8, 128), F32),
            jax.ShapeDtypeStruct((16, 1024), F32),
            jax.ShapeDtypeStruct((1024, 128), F32),
            jax.ShapeDtypeStruct((8, 512), F32),
        ),
        in_specs=[vmem] * 6,
        out_specs=[vmem] * 5,
        scratch_shapes=[pltpu.VMEM(shape, kind) for shape, kind in SCRATCH]
        + [pltpu.SemaphoreType.DMA((SLOTS,)), pltpu.SemaphoreType.DMA((SLOTS,))],
        compiler_params=pltpu.CompilerParams(
            collective_id=0, has_side_effects=True, vmem_limit_bytes=62 * 2**20
        ),
    )(features, w_first, w_second, heads, rein, rates)
    advantages = advantages[:, :, :96].transpose(1, 0, 2).reshape(8, 384)
    count = features.shape[0] * lax.axis_size("batch") * 8
    return advantages, 0.5 * loss[0, 0] / count, grad_first, grad_second, grad_head.T


def solution(mesh):
    placed = (
        P("batch", None),
        P("batch", "hidden"),
        P("hidden", "batch"),
        P("hidden", None),
        P(None, "batch"),
        P(),
        P(),
        P("batch"),
    )
    return jax.shard_map(
        shards,
        mesh=mesh,
        in_specs=placed,
        out_specs=(
            P(None, "batch"),
            P(),
            P("batch", "hidden"),
            P("hidden", "batch"),
            P("hidden", None),
        ),
        check_vma=False,
    )
```

time: 451 us -> 165 us (0.37)
  waiting for transfers between devices: 336 us -> 0 us
  Pallas kernels: 0 us -> 153 us
  starting transfers between devices: 42.3 us -> 0 us
  matrix products: 30.4 us -> 0 us
  between operations: 16.8 us -> 2.47 us
  local copies, waits for them, and re-layouts: 16.5 us -> 8.08 us
  other arithmetic: 8.07 us -> 1.24 us
    all_gather x3 -> x0, waiting for transfers between devices: 178 us -> none  [the longest x1 82.7 us: shards(): lax.all_gather(w_second, 'batch', axis=1, tiled=True)]
    pallas_call x0 -> x1, Pallas kernels: none -> 153 us  [shards(): pl.pallas_call(kernel, out_shape=(jax.ShapeDtypeStruct((4, 8, 128), F32),...]
    reduce_scatter x2 -> x0, waiting for transfers between devices: 93.7 us -> none  [the longest x1 55.6 us: shards(): lax.psum_scatter(contract(columns, hidden_first, 0, 0).astype(jnp.bfloat1...]
    all_to_all x5 -> x0, waiting for transfers between devices: 59.8 us -> none  [the longest x4 30.9 us: sent_to_all(): lax.all_to_all(jnp.broadcast_to(array[None], (length, *array.shape)), axi...]
    all_to_all x5 -> x0, starting transfers between devices: 31.6 us -> none  [the longest x4 27.1 us: sent_to_all(): lax.all_to_all(jnp.broadcast_to(array[None], (length, *array.shape)), axi...]
    dot_general x7 -> x0, matrix products: 30.4 us -> none  [the longest x4 20.2 us: contract(): lax.dot_general(left, right, (((left_dim,), (right_dim,)), ((), ())), pre...]
    ppermute x2 -> x0, starting transfers between devices: 10.4 us -> none  [passed_along(): lax.ppermute(value, axis, [(source, source + steps) for source in range(i...]
    slice x70 -> x1, local copies, waits for them, and re-layouts: 6.46 us -> 1.21 us  [shards(): loss[0, 0]]
  transfers between devices with their start and end apart: 12 -> 0, of which waited for: 11 -> 0; matrix products, arithmetic and copies ran while one was open for 4% -> 0% of each run, Pallas kernels for 0% -> 0%
where the time goes in v1:
time: 165 us
  Pallas kernels  153 us (93%)
  local copies, waits for them, and re-layouts  8.08 us (5%)
  between operations  2.47 us (1%)
    pallas_call x1, Pallas kernels, shards(): pl.pallas_call(kernel, out_shape=(jax.ShapeDtypeStruct((4, 8, 128), F32),...  153 us
    unnamed x17, local copies, waits for them, and re-layouts  4.6 us

profile of v1, /device:TPU:1, one launch (start us, length us, event | category | flops | bytes accessed | tf_op | source)
XLA Modules:
  0.0 165.0 jit_solution(12936441847786718541)
XLA Ops:
  0.6 0.0 copy-start.5
  0.6 0.0 copy-start.6
  0.7 0.0 copy-start.4
  0.7 0.6 copy-done.5
  1.3 0.0 copy-done.6
  1.3 0.0 copy-done.4
  1.3 0.1 reshape.28
  1.4 0.7 broadcast_in_dim.2.dt
  2.1 0.0 copy-start.3
  2.1 0.7 copy-done.3
  2.8 0.0 copy-start.2
  2.8 0.6 convert_bitcast_fusion.whin
  3.4 0.1 copy-done.2
  3.5 0.1 reshape.27
  3.6 0.6 pad_maximum_fusion.rein
  4.2 153.3 %shard_map.119 = (f32[4,8,128]{2,1,0:T(8,128)}, f32[8,128]{1,0:T(8,128)}, f32[16,1024]{1,0:T(8,128)}, f32[1024,128]{1,0:T(8,128)}, f32[8,512]{1,0:T(8,128)}) custom-call(bf16[384,512]{1,0:T(8,128)(2,1)} %feat.1, bf16[16,1024]{1,0:T(8,128)(2,1)} %w1in.1, bf16[1024,128]{1,0:T(8,128)(2,1)} %w2in.1, f32[8,512]{1,0:T(8,128)} %convert_bitcast_fusion.whin, ...), custom_call_target="tpu_custom_call" | custom-call | tf_op jit(solution)/shard_map/pallas_call | solution.py:700
  157.5 0.0 copy-start
  157.5 1.2 slice.7
  159.4 0.7 slice_bitcast_fusion
  160.1 0.7 reshape.29
  160.8 0.0 copy-done
  160.8 0.6 copy.18
  161.4 0.0 copy-start.1
  161.4 1.9 %copy.19 = f32[1024,128]{1,0:T(8,128)} copy(f32[1024,128]{1,0:T(8,128)} %get-tuple-element.23) | data formatting | bytes 1048576
  163.3 0.0 copy-done.1
  163.3 0.6 copy.20
  (7 shorter events, 0.0 us)
Async XLA Ops:
  0.6 0.7 copy-start.5
  0.6 0.7 copy-start.6
  0.7 0.7 copy-start.4
  2.1 0.7 copy-start.3
  2.8 0.7 copy-start.2
  157.5 3.3 %copy-start = (f32[16,1024]{1,0:T(8,128)S(1)}, f32[16,1024]{1,0:T(8,128)}, u32[]{:S(2)}) copy-start(f32[16,1024]{1,0:T(8,128)} %get-tuple-element.22) | copy-start | bytes 196612
  161.4 1.9 %copy-start.1 = (f32[8,512]{1,0:T(8,128)S(1)}, f32[8,512]{1,0:T(8,128)}, u32[]{:S(2)}) copy-start(f32[8,512]{1,0:T(8,128)} %get-tuple-element.14) | copy-start | bytes 49156

commit v2 on v1

v2 whole, which is shorter than its diff:
```python
import functools

import jax
import jax.numpy as jnp
from jax import lax
from jax.experimental import pallas as pl
from jax.experimental.pallas import tpu as pltpu
from jax.sharding import PartitionSpec as P

BF16, F32 = jnp.bfloat16, jnp.float32
MESH = pl.DeviceIdType.MESH
SLOTS = 240
LOW, HIGH = pl.ds(0, 512), pl.ds(512, 512)


def dot(left, right, dims=((1,), (0,))):
    return lax.dot_general(left, right, (dims, ((), ())), preferred_element_type=F32)


def mod(value, count):
    return lax.rem(value + count, count)


def lane(dx):
    return pl.ds(dx * 128, 128)


class Links:
    def __init__(self, sent, came):
        self.sent, self.came, self.used, self.open = sent, came, 0, []

    def take(self):
        self.used += 1
        return self.used - 1

    def make(self, src, dst, to, k, k_came=None):
        return pltpu.make_async_remote_copy(
            src_ref=src,
            dst_ref=dst,
            send_sem=self.sent.at[k],
            recv_sem=self.came.at[k if k_came is None else k_came],
            device_id=to,
            device_id_type=MESH,
        )

    def push(self, src, dst, to, land=None):
        k = self.take()
        copy = self.make(src, dst, to, k)
        copy.start()
        self.open.append(copy)
        return copy if land is None else self.make(land, land, to, k)

    def drain(self):
        for copy in self.open:
            copy.wait_send()
        self.open = []


def kernel(
    feat, w1in, w2in, whin, reward_in, number_in, discount_in, trace_in,
    adv_o, loss_o, g1_o, g2_o, gh_o,
    F, FT, W1, W2, WHB, WH, RE, HF, HFT, SP, PS, RA, RB, RL, RR, RZ, PRE, SL2, H2,
    V, ADV, S, BACK, G2, XA, XB, XL, XR, ZA, ZB, ZL, ZR, BKS, BKR, SF,
    G1, YA, YB, YL, YR, UA, UB, UL, UR, GF, GT, GHP, GR, GS, GZ, GX, GY, GC, GH,
    WHS, RWS, EPS, WIN, sent, came, local,
):
    b, j = lax.axis_index("batch"), lax.axis_index("hidden")
    c, m = lax.rem(b, 2), lax.div(b, 2)
    zh, x = lax.rem(m, 4), lax.div(m, 4)
    y, zl = lax.rem(j, 4), lax.div(j, 4)
    r = y * 2 + zl
    link = Links(sent, came)
    push = link.push

    def at(dx=0, dz=0, dc=0, dy=0, dl=0):
        bb = (mod(x + dx, 4) * 4 + mod(zh + dz, 4)) * 2 + mod(c + dc, 2)
        return bb, mod(zl + dl, 2) * 4 + mod(y + dy, 4)

    def beside(step, dc, dy, dl):
        bb = mod(m + step, 16) * 2 + mod(c + dc, 2)
        return bb, mod(zl + dl, 2) * 4 + mod(y + dy, 4)

    peers = [(dc, dy, dl) for dc in range(2) for dy in range(4) for dl in range(2)]

    loads = [
        pltpu.make_async_copy(src, dst, local.at[k])
        for k, (src, dst) in enumerate(
            (
                (w1in, WIN),
                (w2in, W2.at[0, :, lane(0)]),
                (feat, F.at[c]),
                (whin, WHS),
                (reward_in, RWS),
                (number_in, EPS),
            )
        )
    ]
    for load in loads:
        load.start()

    barrier = pltpu.get_barrier_semaphore()
    partners = [at(dc=dc, dy=dy, dl=dl) for dc, dy, dl in peers[1:]]
    partners += [at(dx=d) for d in (1, 2, 3)] + [at(dz=d) for d in (1, 2, 3)]
    partners += [beside(step, *peer) for step in (1, -1) for peer in peers]
    for partner in partners:
        pl.semaphore_signal(barrier, inc=1, device_id=partner, device_id_type=MESH)
    for load in loads:
        load.wait()
    blank = jnp.zeros((8, 32), F32)
    WHB[j] = WHS[...].astype(F32)
    for i in range(4):
        reward = RWS[:, i * 96 : (i + 1) * 96]
        number = jnp.broadcast_to(EPS[:, i * 96 : (i + 1) * 96].astype(F32), (8, 96))
        RE[c, 0, i] = jnp.concatenate([reward, blank], axis=1)
        RE[c, 1, i] = jnp.concatenate([number, blank], axis=1)
    pl.semaphore_wait(barrier, len(partners))

    mine, theirs = (
        pl.ds(pl.multiple_of(side * 512, 512), 512) for side in (c, 1 - c)
    )
    w1pair = push(WIN.at[:, theirs], W1.at[x, zh, c], at(dc=1), W1.at[x, zh, 1 - c])
    W1[x, zh, c] = WIN[:, mine]

    def w1_sides(zs):
        own = W1.at[x, zs]
        return [push(own, own, at(dx=dx), W1.at[mod(x - dx, 4), zs]) for dx in (1, 3)]

    def w1_across(zs, sides):
        out = []
        for dx, side in ((1, 0), (3, 1)):
            sides[side].wait_recv()
            part = W1.at[mod(x - dx, 4), zs, side]
            out.append(push(part, part, at(dx=dx), W1.at[mod(x + 2, 4), zs, side]))
        return out

    w2x = {}

    def w2_to(dz, half, dx):
        key = (dz, 4 - dx, 0 if half is LOW else 1)
        w2x[key] = push(
            W2.at[dz, half, lane(0)], W2.at[dz, half, lane(4 - dx)], at(dx=dx)
        )

    def w2_side(dz, half):
        near = 1 if half is LOW else 3
        w2_to(dz, half, near)
        w2_to(dz, half, 4 - near)

    def w2_across(dz):
        w2x[dz, 3, 0].wait_recv()
        w2x[dz, 2, 0] = push(
            W2.at[dz, LOW, lane(3)], W2.at[dz, LOW, lane(2)], at(dx=1)
        )
        w2x[dz, 1, 1].wait_recv()
        w2x[dz, 2, 1] = push(
            W2.at[dz, HIGH, lane(1)], W2.at[dz, HIGH, lane(2)], at(dx=3)
        )

    def w2_rest(dz, keys=((3, 1), (1, 0), (2, 0), (2, 1))):
        for key in keys:
            w2x[(dz, *key)].wait_recv()

    def w2_z(half, dz):
        return push(W2.at[0, half, lane(0)], W2.at[4 - dz, half, lane(0)], at(dz=dz))

    first, second, w1z, w1x, w1far = [], [], {}, {}, {}

    def w1_start():
        w1pair.wait_recv()
        own = W1.at[x, zh]
        for dz in (1, 3, 2):
            w1z[dz] = push(own, own, at(dz=dz), W1.at[x, mod(zh - dz, 4)])
        w1x[0] = w1_sides(zh)

    def w1_from_z(dz):
        w1z[dz].wait_recv()
        w1x[dz] = w1_sides(mod(zh - dz, 4))

    def w1_far(dz):
        w1far[dz] = w1_across(mod(zh - dz, 4), w1x[dz])

    def w1_done():
        for dz in (0, 1, 3, 2):
            for copy in w1far[dz]:
                copy.wait_recv()

    w1_start()
    w2_to(0, LOW, 1)
    w2_to(0, HIGH, 3)
    first += [w2_z(LOW, 1), w2_z(HIGH, 3)]
    second += [w2_z(HIGH, 1), w2_z(LOW, 3)]
    feat_in = push(F.at[c], F.at[c], at(dc=1), F.at[1 - c])
    w1_from_z(1)
    w1_from_z(3)
    w1_far(0)
    w1_from_z(2)
    w2_to(0, HIGH, 1)
    w2_to(0, LOW, 3)
    re_in = push(RE.at[c], RE.at[c], at(dc=1), RE.at[1 - c])
    re_sem = [link.take() for _ in range(2)]
    re_to = [
        link.make(RE.at[c], RE.at[2], beside(-1, dc, 0, 0), re_sem[dc], re_sem[0])
        for dc in range(2)
    ]

    @pl.when(c == 0)
    def _():
        for copy in re_to:
            copy.start()

    wh_in = [
        push(WHB.at[j], WHB.at[j], at(dy=dy, dl=dl), WHB.at[mod(zl - dl, 2) * 4 + mod(y - dy, 4)])
        for dc, dy, dl in peers[1:8]
    ]

    w1_far(1)
    w1_far(3)
    w1_far(2)
    w2_across(0)
    w2_z2 = []

    def w2_first():
        first[0].wait_recv()
        w2_z2.append(push(W2.at[3, LOW, lane(0)], W2.at[2, LOW, lane(0)], at(dz=1)))
        w2_side(3, LOW)
        first[1].wait_recv()
        w2_z2.append(push(W2.at[1, HIGH, lane(0)], W2.at[2, HIGH, lane(0)], at(dz=3)))
        w2_side(1, HIGH)

    def w2_second():
        second[0].wait_recv()
        w2_side(3, HIGH)
        second[1].wait_recv()
        w2_side(1, LOW)

    def w2_third():
        w2_z2[0].wait_recv()
        w2_side(2, LOW)
        w2_z2[1].wait_recv()
        w2_side(2, HIGH)

    w2_first()
    feat_in.wait_recv()
    w1_done()
    hf_in = []

    def layer_one():
        for n in range(2):
            cols = pl.ds(n * 256, 256)
            into = pl.ds(pl.multiple_of(c * 512 + n * 256, 256), 256)
            there = pl.ds(pl.multiple_of((1 - c) * 512 + n * 256, 256), 256)
            weights = W1[:, :, :, :, cols].reshape(512, 256)
            SP[:, cols] = dot(F[...].reshape(768, 512), weights)

            @pl.loop(0, 12)
            def _(i):
                rows = pl.ds(pl.multiple_of(i * 64, 64), 64)
                value = SP[rows, cols]
                gate = 1.0 / (1.0 + jnp.exp(-value))
                HF[rows, into] = (value * gate).astype(BF16)
                SP[rows, cols] = gate * (1.0 + value * (1.0 - gate))

            src = HF.at[:, into]
            hf_in.append(push(src, src, at(dc=1), HF.at[:, there]))

    layer_one()
    w2_second()

    def product(dz, part=None):
        for n in range(2) if part is None else (part,):
            out = dot(HF[...], W2[dz, :, pl.ds(n * 256, 256)])
            into = pl.ds(dz * 512 + n * 256, 256)
            PS[:, :, into] = out.astype(BF16).reshape(8, 96, 256)

    up, down, over = mod(y + 1, 4), mod(y - 1, 4), mod(y + 2, 4)
    came_rs = {}

    def lanes(dz, part):
        if part is None:
            return pl.ds(dz * 512, 512), pl.ds(0, 512)
        return pl.ds(dz * 512 + part * 256, 256), pl.ds(part * 256, 256)

    def scatter_a(dz, part=None):
        wide, here = lanes(dz, part)
        came_rs[dz, part] = [
            push(PS.at[over * 2, :, wide], RA.at[dz, :, here], at(dy=1)),
            push(PS.at[over * 2 + 1, :, wide], RB.at[dz, :, here], at(dy=3)),
            push(PS.at[up * 2 + 1, :, wide], RL.at[dz, 1, :, here], at(dy=1)),
            push(PS.at[down * 2, :, wide], RR.at[dz, 0, :, here], at(dy=3)),
        ]

    def scatter_b(dz, part=None):
        wide, here = lanes(dz, part)
        for got, buf, row, dst, dy in (
            (came_rs[dz, part][0], RA, up * 2, RL.at[dz, 0, :, here], 1),
            (came_rs[dz, part][1], RB, down * 2 + 1, RR.at[dz, 1, :, here], 3),
        ):
            got.wait_recv()
            total = PS[row, :, wide].astype(F32) + buf[dz, :, here].astype(F32)
            PS[row, :, wide] = total.astype(BF16)
            came_rs[dz, part].append(push(PS.at[row, :, wide], dst, at(dy=dy)))

    def scatter_c(dz, part=None):
        wide, here = lanes(dz, part)
        for got in came_rs[dz, part][2:]:
            got.wait_recv()

        def total(side):
            return (
                PS[y * 2 + side, :, wide].astype(F32)
                + RL[dz, side, :, here].astype(F32)
                + RR[dz, side, :, here].astype(F32)
            )

        PS[y * 2 + 1 - zl, :, wide] = total(1 - zl).astype(BF16)
        came_rs[dz, part].append(
            push(PS.at[y * 2 + 1 - zl, :, wide], RZ.at[dz, :, here], at(dl=1))
        )
        PRE[:, wide] = total(zl)

    def scatter_d(dz, part=None):
        wide, here = lanes(dz, part)
        came_rs[dz, part][-1].wait_recv()

        @pl.loop(0, 3)
        def _(i):
            rows = pl.ds(pl.multiple_of(i * 32, 32), 32)
            value = PRE[rows, wide] + RZ[dz, rows, here].astype(F32)
            gate = 1.0 / (1.0 + jnp.exp(-value))
            H2[rows, wide] = (value * gate).astype(BF16)
            SL2[rows, wide] = gate * (1.0 + value * (1.0 - gate))

    for got in hf_in:
        got.wait_recv()
    w2_rest(0)
    product(0)
    scatter_a(0)
    w2_across(3)
    w2_across(1)
    w2_third()
    scatter_b(0)

    def transposes():
        @pl.loop(0, 4)
        def _(n):
            cols = pl.ds(pl.multiple_of(n * 256, 256), 256)
            HFT[cols, :] = HF[:, cols].astype(F32).T.astype(BF16)

        @pl.loop(0, 2)
        def _(n):
            cols = pl.ds(pl.multiple_of(n * 256, 256), 256)
            FT[cols, :] = F[:, :, cols].reshape(768, 256).astype(F32).T.astype(BF16)

    transposes()
    w2_rest(3)
    product(3)
    scatter_a(3)
    scatter_c(0)
    w2_rest(1)
    product(1)
    scatter_a(1)
    w2_across(2)
    scatter_b(3)
    for copy in wh_in:
        copy.wait_recv()
    for dz in range(4):
        for dx in range(4):
            mm = mod(x + dx, 4) * 4 + mod(zh + dz, 4)
            group, pair = lax.div(mm, 2), lax.rem(mm, 2)
            even, odd = (
                jnp.where(c == 0, WHB[group, :, lane(2 * p)], WHB[group, :, lane(2 * p + 1)])
                for p in (0, 1)
            )
            WH[:, lane(dz * 4 + dx)] = jnp.where(pair == 0, even, odd).astype(BF16)
    scatter_d(0)
    scatter_b(1)
    w2_rest(2, ((1, 0),))
    product(2, 0)
    scatter_a(2, 0)
    w2_rest(2, ((3, 1), (2, 0), (2, 1)))
    product(2, 1)
    scatter_a(2, 1)
    scatter_c(3)
    scatter_c(1)
    scatter_d(3)
    scatter_b(2, 0)
    scatter_b(2, 1)
    scatter_d(1)
    scatter_c(2, 0)
    scatter_c(2, 1)
    scatter_d(2, 0)
    scatter_d(2, 1)

    own_values = dot(WH[...], H2[...], ((1,), (1,)))
    V[c, r] = jnp.concatenate([own_values, blank], axis=1)
    v_in = []
    for dc, dy, dl in peers[1:]:
        src_r = mod(y - dy, 4) * 2 + mod(zl - dl, 2)
        v_in.append(
            push(V.at[c, r], V.at[c, r], at(dc=dc, dy=dy, dl=dl), V.at[mod(c - dc, 2), src_r])
        )
    v_out, v_next = [], []
    for dc, dy, dl in peers:
        k = link.take()
        src_r = mod(y - dy, 4) * 2 + mod(zl - dl, 2)
        v_out.append(
            link.make(V.at[c, r], V.at[c, 8 + lax.rem(r, 4)], beside(-1, dc, dy, dl), k)
        )
        land = V.at[mod(c - dc, 2), 8 + lax.rem(src_r, 4)]
        v_next.append((src_r, link.make(land, land, beside(-1, dc, dy, dl), k)))

    @pl.when(r < 4)
    def _():
        for copy in v_out:
            copy.start()

    re_in.wait_recv()
    link.make(RE.at[2], RE.at[2], at(dc=1), re_sem[0], re_sem[0]).wait_recv()
    shape = (8, 12 * 128)
    place = lax.rem(lax.broadcasted_iota(jnp.int32, shape, 1), 128)

    def ahead(array, steps):
        return pltpu.roll(array, shape[1] - steps, 1)

    def following(array):
        return jnp.where(place == 95, ahead(array, 33), ahead(array, 1))

    def row_of(kind):
        return jnp.concatenate([RE[i // 4, kind, i % 4] for i in range(12)], axis=1)

    reward, number = row_of(0), row_of(1)
    head_row = lax.broadcasted_iota(jnp.int32, (8, 128), 0)

    def spread(array):
        out = jnp.zeros((8, 128), F32)
        for k in range(8):
            out = jnp.where(head_row == k, array[k], out)
        return out

    rate, decay = spread(discount_in), spread(trace_in)
    discount = jnp.concatenate([rate] * 12, axis=1)
    both = jnp.concatenate([rate * decay] * 12, axis=1)
    keep = jnp.where(following(number) == number, 1.0, 0.0)
    real = place < 96
    factor = jnp.where(real, both * keep, 1.0)
    scale = discount * keep

    for copy in v_in:
        copy.wait_recv()
    for src_r, copy in v_next:

        @pl.when(src_r < 4)
        def _():
            copy.wait_recv()

    value = jnp.concatenate([V[0, i] + V[1, i] for i in range(12)], axis=1)
    total = jnp.where(real, reward + scale * following(value) - value, 0.0)
    step = 1
    while step < shape[1]:
        total = total + factor * ahead(total, step)
        factor = factor * ahead(factor, step)
        step *= 2
    for i in range(12):
        ADV[i] = total[:, i * 128 : (i + 1) * 128]

    own = ADV[r]
    slope_t = (-own[:, :96]).astype(BF16)
    slope = (-own).T[:96, :].astype(BF16)
    own_rows = S.at[r]

    def slope_chunk(dz):
        at_dz = pl.ds(dz * 512, 512)
        own_rows[:, at_dz] = (dot(slope, WH[:, at_dz]) * SL2[:, at_dz]).astype(BF16)

    ag = {}
    pair_r = y * 2 + 1 - zl

    def gather_a(dz, part=None):
        wide, _ = lanes(dz, part)
        src = S.at[r, :, wide]
        ag[dz, part] = {
            "pair": push(src, src, at(dl=1), S.at[pair_r, :, wide]),
            "down": push(src, src, at(dy=1), S.at[down * 2 + zl, :, wide]),
            "up": push(src, src, at(dy=3), S.at[up * 2 + zl, :, wide]),
        }

    def gather_b(dz, part=None):
        wide, _ = lanes(dz, part)
        got = ag[dz, part]
        got["pair"].wait_recv()
        src = S.at[pair_r, :, wide]
        got["down2"] = push(src, src, at(dy=1), S.at[down * 2 + 1 - zl, :, wide])
        got["up2"] = push(src, src, at(dy=3), S.at[up * 2 + 1 - zl, :, wide])

    def gather_c(dz, part=None):
        wide, _ = lanes(dz, part)
        got = ag[dz, part]
        for name in ("down", "up", "down2", "up2"):
            got[name].wait_recv()
        low, high = S.at[down * 2, :, wide], S.at[up * 2 + 1, :, wide]
        got["far"] = [
            push(low, low, at(dy=1), S.at[over * 2, :, wide]),
            push(high, high, at(dy=3), S.at[over * 2 + 1, :, wide]),
        ]

    def gather_d(dz, part=None):
        for got in ag[dz, part]["far"]:
            got.wait_recv()

    def grad_part(dz, part):
        wide, here = lanes(dz, part)

        @pl.loop(0, 2)
        def _(n):
            rows = pl.ds(pl.multiple_of(n * 512, 512), 512)
            G2[dz, rows, here] = dot(HFT[rows, :], S[:, :, wide].reshape(768, 256)).astype(BF16)

    def grad_second(dz, side):
        at_dz = pl.ds(dz * 512, 512)

        @pl.loop(0, 2)
        def _(n):
            rows = pl.ds(pl.multiple_of(side * 512 + n * 256, 256), 256)
            G2[dz, rows, :] = dot(HFT[rows, :], S[:, :, at_dz].reshape(768, 512)).astype(BF16)

    def back_first(dz, start):
        at_dz = pl.ds(dz * 512, 512)

        @pl.loop(0, 4)
        def _(n):
            cols = pl.ds(pl.multiple_of(n * 256, 256), 256)
            part = dot(S[:, :, at_dz].reshape(768, 512), W2[dz, cols, :], ((1,), (1,)))
            BACK[:, cols] = part if start else BACK[:, cols] + part

    gx, halves = {}, (LOW, HIGH)

    def reduce_far(dz, side):
        src = G2.at[dz, halves[side], lane(2)]
        gx[dz, side] = [push(src, (XA, XB)[side].at[dz], at(dx=(1, 3)[side]))]

    def reduce_near(dz, side):
        src = G2.at[dz, halves[side], lane((3, 1)[side])]
        gx[dz, side].append(push(src, (XR, XL)[side].at[dz, side], at(dx=(3, 1)[side])))

    def reduce_a(dz, side):
        reduce_far(dz, side)
        reduce_near(dz, side)

    def reduce_b(dz, side):
        gx[dz, side][0].wait_recv()
        dx, half = (1, 3)[side], halves[side]
        block = G2[dz, half, lane(dx)].astype(F32) + (XA, XB)[side][dz].astype(F32)
        G2[dz, half, lane(dx)] = block.astype(BF16)
        src = G2.at[dz, half, lane(dx)]
        gx[dz, side].append(push(src, (XL, XR)[side].at[dz, side], at(dx=dx)))

    def reduce_c(dz, side, into=None):
        half = halves[side]
        for got in gx[dz, side][1:]:
            got.wait_recv()
        block = (
            G2[dz, half, lane(0)].astype(F32)
            + XL[dz, side].astype(F32)
            + XR[dz, side].astype(F32)
        )
        if into is None:
            G2[dz, half, lane(0)] = block.astype(BF16)
        else:
            into[half, :] = block

    z_far, z_in = [], []

    def reduce_z(dz, side):
        half = halves[side]
        src = G2.at[dz, half, lane(0)]
        if dz == 2:
            z_far.append(push(src, (ZA, ZB)[side], at(dz=(1, 3)[side])))
            return
        if (dz, side) in ((1, 0), (3, 1)):
            z_far[side].wait_recv()
            block = G2[dz, half, lane(0)].astype(F32) + (ZA, ZB)[side][...].astype(F32)
            G2[dz, half, lane(0)] = block.astype(BF16)
        z_in.append(push(src, (ZL if dz == 1 else ZR).at[side], at(dz=dz)))

    slope_chunk(2)
    gather_a(2, 1)
    gather_a(2, 0)
    slope_chunk(1)
    gather_a(1)
    slope_chunk(3)
    slope_chunk(0)
    gather_b(2, 1)
    gather_b(2, 0)
    gather_a(3)

    for i in range(4):
        adv_o[i] = ADV[4 * c + i]
    small = lax.broadcasted_iota(jnp.int32, (8, 128), 1) < 96
    own_loss = jnp.where(small, own * own, 0.0)
    head = dot(slope_t, H2[...])
    for dz in range(4):
        for dx in range(4):
            mm = mod(x + dx, 4) * 4 + mod(zh + dz, 4)
            GHP[lax.div(mm, 2), lax.rem(mm, 2)] = head[:, (dz * 4 + dx) * 128 :][:, :128]
    for g in range(8):
        GHP[g, 2] = own_loss
    gather_c(2, 1)
    gather_c(2, 0)
    gather_b(1)
    gather_a(0)
    gh_in = []
    for dc, dy, dl in peers[1:8]:
        to_j = mod(zl + dl, 2) * 4 + mod(y + dy, 4)
        from_j = mod(zl - dl, 2) * 4 + mod(y - dy, 4)
        gh_in.append(push(GHP.at[to_j], GR.at[j], at(dy=dy, dl=dl), GR.at[from_j]))
    GR[j] = GHP[j]
    gather_d(2, 1)
    grad_part(2, 1)
    reduce_far(2, 0)
    reduce_far(2, 1)
    reduce_near(2, 0)
    gather_d(2, 0)
    grad_part(2, 0)
    reduce_near(2, 1)
    gather_c(1)
    gather_b(3)
    gather_b(0)
    back_first(2, True)
    reduce_b(2, 0)
    reduce_b(2, 1)
    gather_d(1)
    grad_second(1, 1)
    reduce_a(1, 1)
    gather_c(3)
    back_first(1, False)
    gather_c(0)
    gather_d(3)
    grad_second(3, 0)
    reduce_a(3, 0)
    reduce_b(1, 1)
    grad_second(3, 1)
    reduce_a(3, 1)
    grad_second(1, 0)
    reduce_a(1, 0)
    reduce_c(2, 0)
    reduce_z(2, 0)
    reduce_c(2, 1)
    reduce_z(2, 1)
    reduce_b(3, 0)
    back_first(3, False)
    gather_d(0)
    back_first(0, False)

    @pl.loop(0, 12)
    def _(i):
        rows = pl.ds(pl.multiple_of(i * 64, 64), 64)
        BKS[rows, :] = BACK[rows, theirs].astype(BF16)

    back_in = push(BKS, BKR, at(dc=1))
    reduce_b(3, 1)
    reduce_c(1, 1)
    reduce_z(1, 1)
    back_in.wait_recv()

    @pl.loop(0, 12)
    def _(i):
        rows = pl.ds(pl.multiple_of(i * 64, 64), 64)
        back = BACK[rows, mine] + BKR[rows, :].astype(F32)
        SF[rows, :] = (back * SP[rows, :]).astype(BF16)

    @pl.loop(0, 2)
    def _(n):
        rows = pl.ds(pl.multiple_of(n * 256, 256), 256)
        part = dot(FT[rows, :], SF[...]).astype(BF16)
        G1[pl.ds(2 * n, 2)] = part.reshape(2, 4, 32, 512)

    lo, hi = pl.ds(0, 16), pl.ds(16, 16)
    x1, x3, x2 = mod(x + 1, 4), mod(x - 1, 4), mod(x + 2, 4)
    z1, z3, z2 = mod(zh + 1, 4), mod(zh - 1, 4), mod(zh + 2, 4)
    yin = [
        push(G1.at[x2, :, lo], YA, at(dx=1)),
        push(G1.at[x2, :, hi], YB, at(dx=3)),
        push(G1.at[x1, :, hi], YL.at[1], at(dx=1)),
        push(G1.at[x3, :, lo], YR.at[0], at(dx=3)),
    ]
    reduce_b(1, 0)
    grad_second(0, 0)
    grad_second(0, 1)
    reduce_c(3, 0)
    reduce_z(3, 0)

    def sums_y():
        for got, buf, row, half, dst, dx in (
            (yin[0], YA, x1, lo, YL.at[0], 1),
            (yin[1], YB, x3, hi, YR.at[1], 3),
        ):
            got.wait_recv()
            block = G1[row, :, half].astype(F32) + buf[...].astype(F32)
            G1[row, :, half] = block.astype(BF16)
            yin.append(push(G1.at[row, :, half], dst, at(dx=dx)))

    sums_y()
    reduce_a(0, 0)
    reduce_a(0, 1)
    for got in gh_in:
        got.wait_recv()
    GS[...] = functools.reduce(jnp.add, [GR[i] for i in range(8)])
    gz_in = [push(GS, GZ.at[d - 1], at(dz=d)) for d in (1, 2, 3)]
    reduce_c(3, 1)
    reduce_z(3, 1)
    reduce_c(1, 0)
    reduce_z(1, 0)
    for got in yin[2:]:
        got.wait_recv()
    for side, half in ((0, lo), (1, hi)):
        block = G1[x, :, half].astype(F32) + YL[side].astype(F32) + YR[side].astype(F32)
        G1[x, :, half] = block.astype(BF16)
    uin = [
        push(G1.at[x, z2, lo], UA, at(dz=1)),
        push(G1.at[x, z2, hi], UB, at(dz=3)),
        push(G1.at[x, z1, hi], UL.at[1], at(dz=1)),
        push(G1.at[x, z3, lo], UR.at[0], at(dz=3)),
    ]
    reduce_b(0, 0)
    reduce_b(0, 1)
    for got in gz_in:
        got.wait_recv()
    GY[...] = GS[...] + GZ[0] + GZ[1] + GZ[2]
    gxs_in = [push(GY, GX.at[d - 1], at(dx=d)) for d in (1, 2, 3)]
    for got, buf, row, half, dst, dz in (
        (uin[0], UA, z1, lo, UL.at[0], 1),
        (uin[1], UB, z3, hi, UR.at[1], 3),
    ):
        got.wait_recv()
        block = G1[x, row, half].astype(F32) + buf[...].astype(F32)
        G1[x, row, half] = block.astype(BF16)
        uin.append(push(G1.at[x, row, half], dst, at(dz=dz)))
    for got in gxs_in:
        got.wait_recv()
    heads = GY[...] + GX[0] + GX[1] + GX[2]
    GH[...] = heads
    gc_in = push(GH, GC, at(dc=1))
    for got in uin[2:]:
        got.wait_recv()
    for side, half in ((0, lo), (1, hi)):
        GF[side] = (
            G1[x, zh, half].astype(F32) + UL[side].astype(F32) + UR[side].astype(F32)
        )
    gt_in = push(GF.at[1 - c], GT, at(dc=1))
    gc_in.wait_recv()
    other = GC[...]
    loss_o[...] = jnp.broadcast_to(jnp.sum(heads[2]), (8, 128))
    for i in range(2):
        gh_o[:, lane(2 * i)] = jnp.where(c == 0, heads[i], other[i])
        gh_o[:, lane(2 * i + 1)] = jnp.where(c == 0, other[i], heads[i])
    reduce_c(0, 0, g2_o)
    reduce_c(0, 1, g2_o)
    for got in z_in:
        got.wait_recv()
    for side, half in ((0, LOW), (1, HIGH)):
        g2_o[half, :] = g2_o[half, :] + ZL[side].astype(F32) + ZR[side].astype(F32)
    gt_in.wait_recv()
    kept, brought = GF[c], GT[...]
    g1_o[:, LOW] = jnp.where(c == 0, kept, brought)
    g1_o[:, HIGH] = jnp.where(c == 0, brought, kept)

    link.drain()

    @pl.when(c == 0)
    def _():
        for copy in re_to:
            copy.wait_send()

    @pl.when(r < 4)
    def _():
        for copy in v_out:
            copy.wait_send()


SCRATCH = [
    ((2, 384, 512), BF16), ((512, 768), BF16), ((4, 4, 2, 16, 512), BF16),
    ((4, 1024, 512), BF16), ((8, 8, 512), F32), ((8, 2048), BF16), ((3, 2, 4, 8, 128), F32),
    ((768, 1024), BF16), ((1024, 768), BF16), ((768, 512), F32), ((8, 96, 2048), BF16),
    ((4, 96, 512), BF16), ((4, 96, 512), BF16), ((4, 2, 96, 512), BF16),
    ((4, 2, 96, 512), BF16), ((4, 96, 512), BF16), ((96, 2048), F32), ((96, 2048), F32),
    ((96, 2048), BF16), ((2, 12, 8, 128), F32), ((12, 8, 128), F32), ((8, 96, 2048), BF16),
    ((768, 1024), F32), ((4, 1024, 512), BF16), ((4, 512, 128), BF16), ((4, 512, 128), BF16),
    ((4, 2, 512, 128), BF16), ((4, 2, 512, 128), BF16), ((512, 128), BF16),
    ((512, 128), BF16), ((2, 512, 128), BF16), ((2, 512, 128), BF16), ((768, 512), BF16),
    ((768, 512), BF16), ((768, 512), BF16), ((4, 4, 32, 512), BF16), ((4, 16, 512), BF16),
    ((4, 16, 512), BF16), ((2, 4, 16, 512), BF16), ((2, 4, 16, 512), BF16), ((16, 512), BF16),
    ((16, 512), BF16), ((2, 16, 512), BF16), ((2, 16, 512), BF16), ((2, 16, 512), F32),
    ((16, 512), F32), ((8, 3, 8, 128), F32), ((8, 3, 8, 128), F32), ((3, 8, 128), F32),
    ((3, 3, 8, 128), F32), ((3, 3, 8, 128), F32), ((3, 8, 128), F32), ((3, 8, 128), F32),
    ((3, 8, 128), F32), ((8, 512), BF16), ((8, 384), F32), ((1, 384), jnp.int32),
    ((16, 1024), BF16),
]


def finish(adv, loss, g1, g2, gh, adv_o, loss_o, g1_o, g2_o, gh_o):
    adv_o[...] = jnp.concatenate([adv[i][:, :96] for i in range(4)], axis=1)
    loss_o[0, 0] = loss[0, 0] * (0.5 / 98304)
    g1_o[...] = g1[...]
    g2_o[...] = g2[...]
    gh_o[...] = gh[...]


def shards(features, w_first, w_second, w_head, rewards, discount, trace, episode):
    vmem = pl.BlockSpec(memory_space=pltpu.VMEM)
    smem = pl.BlockSpec(memory_space=pltpu.SMEM)
    hbm = pl.BlockSpec(memory_space=pltpu.HBM)
    shapes = ((16, 1024), (1024, 128), (8, 512))
    parts = pl.pallas_call(
        kernel,
        out_shape=[
            jax.ShapeDtypeStruct(shape, F32) for shape in ((4, 8, 128), (8, 128), *shapes)
        ],
        in_specs=[hbm] * 6 + [smem] * 2,
        out_specs=[vmem] * 5,
        scratch_shapes=[pltpu.VMEM(shape, kind) for shape, kind in SCRATCH]
        + [pltpu.SemaphoreType.DMA((count,)) for count in (SLOTS, SLOTS, 6)],
        compiler_params=pltpu.CompilerParams(
            collective_id=0, has_side_effects=True, vmem_limit_bytes=62 * 2**20
        ),
    )(
        features, w_first, w_second, w_head.T, rewards, episode.reshape(1, -1),
        discount, trace,
    )
    advantages, loss, grad_first, grad_second, grad_head = pl.pallas_call(
        finish,
        out_shape=[
            jax.ShapeDtypeStruct(shape, F32) for shape in ((8, 384), (1, 1), *shapes)
        ],
        in_specs=[vmem, smem, vmem, vmem, vmem],
        out_specs=[vmem, smem, vmem, vmem, vmem],
    )(*parts)
    return advantages, loss[0, 0], grad_first, grad_second, grad_head.T


def solution(mesh):
    placed = (
        P("batch", None),
        P("batch", "hidden"),
        P("hidden", "batch"),
        P("hidden", None),
        P(None, "batch"),
        P(),
        P(),
        P("batch"),
    )
    return jax.shard_map(
        shards,
        mesh=mesh,
        in_specs=placed,
        out_specs=(
            P(None, "batch"),
            P(),
            P("batch", "hidden"),
            P("hidden", "batch"),
            P("hidden", None),
        ),
        check_vma=False,
    )
```

time: 165 us -> 150 us (0.909)
  local copies, waits for them, and re-layouts: 8.08 us -> 1.25 us
  Pallas kernels: 153 us -> 148 us
  between operations: 2.47 us -> 0.8 us
    pallas_call x1 -> x2, Pallas kernels: 153 us -> 148 us  [the longest x1 146 us: shards(): pl.pallas_call(kernel, out_shape=[jax.ShapeDtypeStruct(shape, F32) for sh...]
    unnamed x17 -> x0, local copies, waits for them, and re-layouts: 4.6 us -> none
where the time goes in v2:
time: 150 us
  Pallas kernels  148 us (99%)
    pallas_call x1, Pallas kernels, shards(): pl.pallas_call(kernel, out_shape=[jax.ShapeDtypeStruct(shape, F32) for sh...  146 us

profile of v2, /device:TPU:1, one launch (start us, length us, event | category | flops | bytes accessed | tf_op | source)
XLA Modules:
  0.0 150.0 jit_solution(2279211978191844826)
XLA Ops:
  0.6 1.2 reshape.13.number_in
  1.9 146.0 %shard_map.119 = (f32[4,8,128]{2,1,0:T(8,128)}, f32[8,128]{1,0:T(8,128)}, f32[16,1024]{1,0:T(8,128)}, f32[1024,128]{1,0:T(8,128)}, f32[8,512]{1,0:T(8,128)}) custom-call(bf16[384,512]{1,0:T(8,128)(2,1)} %feat.1, bf16[16,1024]{1,0:T(8,128)(2,1)} %w1in.1, bf16[1024,128]{1,0:T(8,128)(2,1)} %w2in.1, bf16[8,512]{1,0:T(8,128)(2,1)} %bitcast.3, ...), custom_call_target="tpu_custom_call" | custom-call | tf_op jit(solution)/shard_map/pallas_call | solution.py:813
  147.9 2.0 %shard_map.120 = (f32[8,384]{1,0:T(8,128)}, f32[1,1]{1,0:T(1,128)}, f32[16,1024]{1,0:T(8,128)}, f32[1024,128]{1,0:T(8,128)}, f32[8,512]{1,0:T(8,128)}) custom-call(f32[4,8,128]{2,1,0:T(8,128)} %get-tuple-element.15.adv, f32[8,128]{1,0:T(8,128)} %get-tuple-element.16.loss, f32[16,1024]{1,0:T(8,128)} %get-tuple-element.17.g1, ...), custom_call_target="tpu_custom_call" | custom-call | tf_op jit(solution)/shard_map/pallas_call | solution.py:829

commit v3 on v2

--- a/solution.py
+++ b/solution.py
@@ -188,14 +188,14 @@
     w2_to(0, LOW, 1)
     w2_to(0, HIGH, 3)
     first += [w2_z(LOW, 1), w2_z(HIGH, 3)]
-    second += [w2_z(HIGH, 1), w2_z(LOW, 3)]
     feat_in = push(F.at[c], F.at[c], at(dc=1), F.at[1 - c])
     w1_from_z(1)
+    w2_to(0, HIGH, 1)
+    w2_to(0, LOW, 3)
     w1_from_z(3)
     w1_far(0)
     w1_from_z(2)
-    w2_to(0, HIGH, 1)
-    w2_to(0, LOW, 3)
+    second += [w2_z(HIGH, 1), w2_z(LOW, 3)]
     re_in = push(RE.at[c], RE.at[c], at(dc=1), RE.at[1 - c])
     re_sem = [link.take() for _ in range(2)]
     re_to = [
@@ -359,8 +359,8 @@
     w2_rest(1)
     product(1)
     scatter_a(1)
+    scatter_b(3)
     w2_across(2)
-    scatter_b(3)
     for copy in wh_in:
         copy.wait_recv()
     for dz in range(4):
@@ -631,22 +631,22 @@
     gather_d(1)
     grad_second(1, 1)
     reduce_a(1, 1)
+    grad_second(1, 0)
+    reduce_a(1, 0)
     gather_c(3)
     back_first(1, False)
     gather_c(0)
+    reduce_b(1, 1)
     gather_d(3)
     grad_second(3, 0)
     reduce_a(3, 0)
-    reduce_b(1, 1)
     grad_second(3, 1)
     reduce_a(3, 1)
-    grad_second(1, 0)
-    reduce_a(1, 0)
+    reduce_b(1, 0)
     reduce_c(2, 0)
     reduce_z(2, 0)
     reduce_c(2, 1)
     reduce_z(2, 1)
-    reduce_b(3, 0)
     back_first(3, False)
     gather_d(0)
     back_first(0, False)
@@ -657,9 +657,10 @@
         BKS[rows, :] = BACK[rows, theirs].astype(BF16)
 
     back_in = push(BKS, BKR, at(dc=1))
+    reduce_b(3, 0)
     reduce_b(3, 1)
-    reduce_c(1, 1)
-    reduce_z(1, 1)
+    grad_second(0, 0)
+    grad_second(0, 1)
     back_in.wait_recv()
 
     @pl.loop(0, 12)
@@ -683,9 +684,12 @@
         push(G1.at[x1, :, hi], YL.at[1], at(dx=1)),
         push(G1.at[x3, :, lo], YR.at[0], at(dx=3)),
     ]
-    reduce_b(1, 0)
-    grad_second(0, 0)
-    grad_second(0, 1)
+    reduce_a(0, 0)
+    reduce_a(0, 1)
+    reduce_c(1, 1)
+    reduce_z(1, 1)
+    reduce_c(1, 0)
+    reduce_z(1, 0)
     reduce_c(3, 0)
     reduce_z(3, 0)
 
@@ -700,16 +704,12 @@
             yin.append(push(G1.at[row, :, half], dst, at(dx=dx)))
 
     sums_y()
-    reduce_a(0, 0)
-    reduce_a(0, 1)
     for got in gh_in:
         got.wait_recv()
     GS[...] = functools.reduce(jnp.add, [GR[i] for i in range(8)])
     gz_in = [push(GS, GZ.at[d - 1], at(dz=d)) for d in (1, 2, 3)]
     reduce_c(3, 1)
     reduce_z(3, 1)
-    reduce_c(1, 0)
-    reduce_z(1, 0)
     for got in yin[2:]:
         got.wait_recv()
     for side, half in ((0, lo), (1, hi)):

time: 150 us -> 148 us (0.987)
  Pallas kernels: 148 us -> 146 us
    pallas_call x1, Pallas kernels: 146 us -> 144 us  [shards(): pl.pallas_call(kernel, out_shape=[jax.ShapeDtypeStruct(shape, F32) for sh...]
where the time goes in v3:
time: 148 us
  Pallas kernels  146 us (99%)
    pallas_call x1, Pallas kernels, shards(): pl.pallas_call(kernel, out_shape=[jax.ShapeDtypeStruct(shape, F32) for sh...  144 us

profile of v3, /device:TPU:1, one launch (start us, length us, event | category | flops | bytes accessed | tf_op | source)
XLA Modules:
  0.0 147.7 jit_solution(3490243931535440211)
XLA Ops:
  0.6 1.2 reshape.13.number_in
  1.9 143.7 %shard_map.119 = (f32[4,8,128]{2,1,0:T(8,128)}, f32[8,128]{1,0:T(8,128)}, f32[16,1024]{1,0:T(8,128)}, f32[1024,128]{1,0:T(8,128)}, f32[8,512]{1,0:T(8,128)}) custom-call(bf16[384,512]{1,0:T(8,128)(2,1)} %feat.1, bf16[16,1024]{1,0:T(8,128)(2,1)} %w1in.1, bf16[1024,128]{1,0:T(8,128)(2,1)} %w2in.1, bf16[8,512]{1,0:T(8,128)(2,1)} %bitcast.3, ...), custom_call_target="tpu_custom_call" | custom-call | tf_op jit(solution)/shard_map/pallas_call | solution.py:813
  145.6 2.0 %shard_map.120 = (f32[8,384]{1,0:T(8,128)}, f32[1,1]{1,0:T(1,128)}, f32[16,1024]{1,0:T(8,128)}, f32[1024,128]{1,0:T(8,128)}, f32[8,512]{1,0:T(8,128)}) custom-call(f32[4,8,128]{2,1,0:T(8,128)} %get-tuple-element.15.adv, f32[8,128]{1,0:T(8,128)} %get-tuple-element.16.loss, f32[16,1024]{1,0:T(8,128)} %get-tuple-element.17.g1, ...), custom_call_target="tpu_custom_call" | custom-call | tf_op jit(solution)/shard_map/pallas_call | solution.py:829

commit v4 on v3

--- a/solution.py
+++ b/solution.py
@@ -9,8 +9,12 @@
 
 BF16, F32 = jnp.bfloat16, jnp.float32
 MESH = pl.DeviceIdType.MESH
-SLOTS = 240
-LOW, HIGH = pl.ds(0, 512), pl.ds(512, 512)
+SLOTS, RING = 195, 64
+EDGE = 192
+HALF = (1024 - EDGE) // 2
+LOW, HIGH = pl.ds(0, HALF), pl.ds(HALF, HALF)
+TOP = pl.ds(2 * HALF, EDGE)
+TOPS = (pl.ds(2 * HALF, EDGE // 2), pl.ds(2 * HALF + EDGE // 2, EDGE // 2))
 
 
 def dot(left, right, dims=((1,), (0,))):
@@ -33,27 +37,29 @@
         self.used += 1
         return self.used - 1
 
-    def make(self, src, dst, to, k, k_came=None):
+    def make(self, src, dst, to, k, k_sent):
         return pltpu.make_async_remote_copy(
             src_ref=src,
             dst_ref=dst,
-            send_sem=self.sent.at[k],
-            recv_sem=self.came.at[k if k_came is None else k_came],
+            send_sem=self.sent.at[k_sent],
+            recv_sem=self.came.at[k],
             device_id=to,
             device_id_type=MESH,
         )
 
-    def push(self, src, dst, to, land=None):
-        k = self.take()
-        copy = self.make(src, dst, to, k)
+    def push(self, src, dst, to, land=None, k=None):
+        k = self.take() if k is None else k
+        turn = len(self.open)
+        if turn >= RING:
+            self.open[turn - RING].wait_send()
+        copy = self.make(src, dst, to, k, turn % RING)
         copy.start()
         self.open.append(copy)
-        return copy if land is None else self.make(land, land, to, k)
+        return copy if land is None else self.make(land, land, to, k, 0)
 
     def drain(self):
-        for copy in self.open:
+        for copy in self.open[-RING:]:
             copy.wait_send()
-        self.open = []
 
 
 def kernel(
@@ -62,7 +68,7 @@
     F, FT, W1, W2, WHB, WH, RE, HF, HFT, SP, PS, RA, RB, RL, RR, RZ, PRE, SL2, H2,
     V, ADV, S, BACK, G2, XA, XB, XL, XR, ZA, ZB, ZL, ZR, BKS, BKR, SF,
     G1, YA, YB, YL, YR, UA, UB, UL, UR, GF, GT, GHP, GR, GS, GZ, GX, GY, GC, GH,
-    WHS, RWS, EPS, WIN, sent, came, local,
+    WHS, RWS, EPS, WIN, EZF, EZL, EZR, EXF, EXL, EXR, sent, came, local,
 ):
     b, j = lax.axis_index("batch"), lax.axis_index("hidden")
     c, m = lax.rem(b, 2), lax.div(b, 2)
@@ -184,7 +190,37 @@
             for copy in w1far[dz]:
                 copy.wait_recv()
 
+    edge = {}
+
+    def edge_x1():
+        src = W2.at[0, TOP, lane(0)]
+        edge["x3"] = push(src, W2.at[0, TOP, lane(3)], at(dx=1))
+        edge["x1"] = push(src, W2.at[0, TOP, lane(1)], at(dx=3))
+
+    def edge_x2():
+        edge["x3"].wait_recv()
+        src = W2.at[0, TOPS[0], lane(3)]
+        edge["x2"] = [push(src, W2.at[0, TOPS[0], lane(2)], at(dx=1))]
+        edge["x1"].wait_recv()
+        src = W2.at[0, TOPS[1], lane(1)]
+        edge["x2"].append(push(src, W2.at[0, TOPS[1], lane(2)], at(dx=3)))
+
+    def edge_z1():
+        for got in edge["x2"]:
+            got.wait_recv()
+        src = W2.at[0, TOP]
+        edge["z3"] = push(src, W2.at[3, TOP], at(dz=1))
+        edge["z1"] = push(src, W2.at[1, TOP], at(dz=3))
+
+    edge["z2"] = []
+
+    def edge_z2(dz):
+        edge["z3" if dz == 3 else "z1"].wait_recv()
+        half = TOPS[0 if dz == 3 else 1]
+        edge["z2"].append(push(W2.at[dz, half], W2.at[2, half], at(dz=4 - dz)))
+
     w1_start()
+    edge_x1()
     w2_to(0, LOW, 1)
     w2_to(0, HIGH, 3)
     first += [w2_z(LOW, 1), w2_z(HIGH, 3)]
@@ -194,12 +230,13 @@
     w2_to(0, LOW, 3)
     w1_from_z(3)
     w1_far(0)
+    edge_x2()
     w1_from_z(2)
     second += [w2_z(HIGH, 1), w2_z(LOW, 3)]
     re_in = push(RE.at[c], RE.at[c], at(dc=1), RE.at[1 - c])
-    re_sem = [link.take() for _ in range(2)]
+    re_sem = link.take()
     re_to = [
-        link.make(RE.at[c], RE.at[2], beside(-1, dc, 0, 0), re_sem[dc], re_sem[0])
+        link.make(RE.at[c], RE.at[2], beside(-1, dc, 0, 0), re_sem, RING + dc)
         for dc in range(2)
     ]
 
@@ -208,12 +245,14 @@
         for copy in re_to:
             copy.start()
 
-    wh_in = [
-        push(WHB.at[j], WHB.at[j], at(dy=dy, dl=dl), WHB.at[mod(zl - dl, 2) * 4 + mod(y - dy, 4)])
-        for dc, dy, dl in peers[1:8]
-    ]
+    wh_sem = link.take()
+    for dc, dy, dl in peers[1:8]:
+        push(WHB.at[j], WHB.at[j], at(dy=dy, dl=dl), k=wh_sem)
+    wh_all = WHB.at[pl.ds(0, 7)]
+    wh_in = [link.make(wh_all, wh_all, at(dc=1), wh_sem, 0)]
 
     w1_far(1)
+    edge_z1()
     w1_far(3)
     w1_far(2)
     w2_across(0)
@@ -337,8 +376,17 @@
     scatter_a(0)
     w2_across(3)
     w2_across(1)
+    scatter_b(0)
+    edge_z2(3)
+    w2_rest(3)
+    product(3)
+    scatter_a(3)
     w2_third()
-    scatter_b(0)
+    edge_z2(1)
+    w2_rest(1)
+    product(1)
+    scatter_a(1)
+    scatter_c(0)
 
     def transposes():
         @pl.loop(0, 4)
@@ -352,13 +400,6 @@
             FT[cols, :] = F[:, :, cols].reshape(768, 256).astype(F32).T.astype(BF16)
 
     transposes()
-    w2_rest(3)
-    product(3)
-    scatter_a(3)
-    scatter_c(0)
-    w2_rest(1)
-    product(1)
-    scatter_a(1)
     scatter_b(3)
     w2_across(2)
     for copy in wh_in:
@@ -375,6 +416,8 @@
     scatter_d(0)
     scatter_b(1)
     w2_rest(2, ((1, 0),))
+    for got in edge["z2"]:
+        got.wait_recv()
     product(2, 0)
     scatter_a(2, 0)
     w2_rest(2, ((3, 1), (2, 0), (2, 1)))
@@ -392,22 +435,17 @@
     scatter_d(2, 1)
 
     own_values = dot(WH[...], H2[...], ((1,), (1,)))
-    V[c, r] = jnp.concatenate([own_values, blank], axis=1)
-    v_in = []
+    own_v = V.at[c * 12 + r]
+    V[c * 12 + r] = jnp.concatenate([own_values, blank], axis=1)
+    v_sem = link.take()
     for dc, dy, dl in peers[1:]:
-        src_r = mod(y - dy, 4) * 2 + mod(zl - dl, 2)
-        v_in.append(
-            push(V.at[c, r], V.at[c, r], at(dc=dc, dy=dy, dl=dl), V.at[mod(c - dc, 2), src_r])
+        push(own_v, own_v, at(dc=dc, dy=dy, dl=dl), k=v_sem)
+    v_out = [
+        link.make(
+            own_v, V.at[c * 12 + 8 + lax.rem(r, 4)], beside(-1, *peer), v_sem, RING + 2 + k
         )
-    v_out, v_next = [], []
-    for dc, dy, dl in peers:
-        k = link.take()
-        src_r = mod(y - dy, 4) * 2 + mod(zl - dl, 2)
-        v_out.append(
-            link.make(V.at[c, r], V.at[c, 8 + lax.rem(r, 4)], beside(-1, dc, dy, dl), k)
-        )
-        land = V.at[mod(c - dc, 2), 8 + lax.rem(src_r, 4)]
-        v_next.append((src_r, link.make(land, land, beside(-1, dc, dy, dl), k)))
+        for k, peer in enumerate(peers)
+    ]
 
     @pl.when(r < 4)
     def _():
@@ -415,7 +453,7 @@
             copy.start()
 
     re_in.wait_recv()
-    link.make(RE.at[2], RE.at[2], at(dc=1), re_sem[0], re_sem[0]).wait_recv()
+    link.make(RE.at[2], RE.at[2], at(dc=1), re_sem, 0).wait_recv()
     shape = (8, 12 * 128)
     place = lax.rem(lax.broadcasted_iota(jnp.int32, shape, 1), 128)
 
@@ -445,15 +483,11 @@
     factor = jnp.where(real, both * keep, 1.0)
     scale = discount * keep
 
+    v_all = V.at[pl.ds(0, 23)]
+    v_in = [link.make(v_all, v_all, at(dc=1), v_sem, 0)]
     for copy in v_in:
         copy.wait_recv()
-    for src_r, copy in v_next:
-
-        @pl.when(src_r < 4)
-        def _():
-            copy.wait_recv()
-
-    value = jnp.concatenate([V[0, i] + V[1, i] for i in range(12)], axis=1)
+    value = jnp.concatenate([V[i] + V[12 + i] for i in range(12)], axis=1)
     total = jnp.where(real, reward + scale * following(value) - value, 0.0)
     step = 1
     while step < shape[1]:
@@ -520,7 +554,8 @@
 
         @pl.loop(0, 2)
         def _(n):
-            rows = pl.ds(pl.multiple_of(side * 512 + n * 256, 256), 256)
+            size = (HALF if side == 0 else HALF + EDGE) // 2
+            rows = pl.ds(pl.multiple_of(side * HALF + n * size, 16), size)
             G2[dz, rows, :] = dot(HFT[rows, :], S[:, :, at_dz].reshape(768, 512)).astype(BF16)
 
     def back_first(dz, start):
@@ -567,6 +602,55 @@
             G2[dz, half, lane(0)] = block.astype(BF16)
         else:
             into[half, :] = block
+
+    e_far, e_in, e_x = [], [], []
+
+    def edge_far():
+        for side in (0, 1):
+            src = G2.at[2, TOPS[side], :]
+            e_far.append(push(src, EZF.at[side], at(dz=(1, 3)[side])))
+
+    def edge_near(dz):
+        buf, near, side = (EZL, 1, 0) if dz == 1 else (EZR, 0, 1)
+        e_in.append(push(G2.at[dz, TOPS[near], :], buf.at[near], at(dz=dz)))
+        e_far[side].wait_recv()
+        block = G2[dz, TOPS[side], :].astype(F32) + EZF[side].astype(F32)
+        G2[dz, TOPS[side], :] = block.astype(BF16)
+        e_in.append(push(G2.at[dz, TOPS[side], :], buf.at[side], at(dz=dz)))
+
+    def edge_sum():
+        for got in e_in:
+            got.wait_recv()
+        for side in (0, 1):
+            block = (
+                G2[0, TOPS[side], :].astype(F32)
+                + EZL[side].astype(F32)
+                + EZR[side].astype(F32)
+            )
+            G2[0, TOPS[side], :] = block.astype(BF16)
+            src = G2.at[0, TOPS[side]]
+            e_x.append(push(src.at[:, lane(2)], EXF.at[side], at(dx=(1, 3)[side])))
+            near = (EXR, EXL)[side].at[side]
+            e_x.append(push(src.at[:, lane((3, 1)[side])], near, at(dx=(3, 1)[side])))
+
+    def edge_mid():
+        for side in (0, 1):
+            e_x[2 * side].wait_recv()
+            dx = (1, 3)[side]
+            block = G2[0, TOPS[side], lane(dx)].astype(F32) + EXF[side].astype(F32)
+            G2[0, TOPS[side], lane(dx)] = block.astype(BF16)
+            src = G2.at[0, TOPS[side], lane(dx)]
+            e_x.append(push(src, (EXL, EXR)[side].at[side], at(dx=dx)))
+
+    def edge_end():
+        for k in (1, 3, 4, 5):
+            e_x[k].wait_recv()
+        for side in (0, 1):
+            g2_o[TOPS[side], :] = (
+                G2[0, TOPS[side], lane(0)].astype(F32)
+                + EXL[side].astype(F32)
+                + EXR[side].astype(F32)
+            )
 
     z_far, z_in = [], []
 
@@ -608,11 +692,11 @@
     gather_c(2, 0)
     gather_b(1)
     gather_a(0)
-    gh_in = []
+    gh_sem, gh_all = link.take(), GR.at[pl.ds(0, 7)]
     for dc, dy, dl in peers[1:8]:
         to_j = mod(zl + dl, 2) * 4 + mod(y + dy, 4)
-        from_j = mod(zl - dl, 2) * 4 + mod(y - dy, 4)
-        gh_in.append(push(GHP.at[to_j], GR.at[j], at(dy=dy, dl=dl), GR.at[from_j]))
+        push(GHP.at[to_j], GR.at[j], at(dy=dy, dl=dl), k=gh_sem)
+    gh_in = [link.make(gh_all, gh_all, at(dc=1), gh_sem, 0)]
     GR[j] = GHP[j]
     gather_d(2, 1)
     grad_part(2, 1)
@@ -622,6 +706,7 @@
     gather_d(2, 0)
     grad_part(2, 0)
     reduce_near(2, 1)
+    edge_far()
     gather_c(1)
     gather_b(3)
     gather_b(0)
@@ -635,6 +720,7 @@
     reduce_a(1, 0)
     gather_c(3)
     back_first(1, False)
+    edge_near(1)
     gather_c(0)
     reduce_b(1, 1)
     gather_d(3)
@@ -642,6 +728,7 @@
     reduce_a(3, 0)
     grad_second(3, 1)
     reduce_a(3, 1)
+    edge_near(3)
     reduce_b(1, 0)
     reduce_c(2, 0)
     reduce_z(2, 0)
@@ -658,9 +745,7 @@
 
     back_in = push(BKS, BKR, at(dc=1))
     reduce_b(3, 0)
-    reduce_b(3, 1)
     grad_second(0, 0)
-    grad_second(0, 1)
     back_in.wait_recv()
 
     @pl.loop(0, 12)
@@ -684,8 +769,8 @@
         push(G1.at[x1, :, hi], YL.at[1], at(dx=1)),
         push(G1.at[x3, :, lo], YR.at[0], at(dx=3)),
     ]
-    reduce_a(0, 0)
-    reduce_a(0, 1)
+    reduce_b(3, 1)
+    grad_second(0, 1)
     reduce_c(1, 1)
     reduce_z(1, 1)
     reduce_c(1, 0)
@@ -704,10 +789,16 @@
             yin.append(push(G1.at[row, :, half], dst, at(dx=dx)))
 
     sums_y()
+    reduce_a(0, 0)
+    reduce_a(0, 1)
+    edge_sum()
     for got in gh_in:
         got.wait_recv()
     GS[...] = functools.reduce(jnp.add, [GR[i] for i in range(8)])
-    gz_in = [push(GS, GZ.at[d - 1], at(dz=d)) for d in (1, 2, 3)]
+    gz_sem, gx_sem = link.take(), link.take()
+    for d in (1, 2, 3):
+        push(GS, GZ.at[d - 1], at(dz=d), k=gz_sem)
+    gz_in = [link.make(GZ, GZ, at(dz=1), gz_sem, 0)]
     reduce_c(3, 1)
     reduce_z(3, 1)
     for got in yin[2:]:
@@ -723,10 +814,7 @@
     ]
     reduce_b(0, 0)
     reduce_b(0, 1)
-    for got in gz_in:
-        got.wait_recv()
-    GY[...] = GS[...] + GZ[0] + GZ[1] + GZ[2]
-    gxs_in = [push(GY, GX.at[d - 1], at(dx=d)) for d in (1, 2, 3)]
+    edge_mid()
     for got, buf, row, half, dst, dz in (
         (uin[0], UA, z1, lo, UL.at[0], 1),
         (uin[1], UB, z3, hi, UR.at[1], 3),
@@ -735,6 +823,12 @@
         block = G1[x, row, half].astype(F32) + buf[...].astype(F32)
         G1[x, row, half] = block.astype(BF16)
         uin.append(push(G1.at[x, row, half], dst, at(dz=dz)))
+    for got in gz_in:
+        got.wait_recv()
+    GY[...] = GS[...] + GZ[0] + GZ[1] + GZ[2]
+    for d in (1, 2, 3):
+        push(GY, GX.at[d - 1], at(dx=d), k=gx_sem)
+    gxs_in = [link.make(GX, GX, at(dx=1), gx_sem, 0)]
     for got in gxs_in:
         got.wait_recv()
     heads = GY[...] + GX[0] + GX[1] + GX[2]
@@ -755,14 +849,15 @@
         gh_o[:, lane(2 * i + 1)] = jnp.where(c == 0, other[i], heads[i])
     reduce_c(0, 0, g2_o)
     reduce_c(0, 1, g2_o)
+    edge_end()
     for got in z_in:
         got.wait_recv()
     for side, half in ((0, LOW), (1, HIGH)):
         g2_o[half, :] = g2_o[half, :] + ZL[side].astype(F32) + ZR[side].astype(F32)
     gt_in.wait_recv()
     kept, brought = GF[c], GT[...]
-    g1_o[:, LOW] = jnp.where(c == 0, kept, brought)
-    g1_o[:, HIGH] = jnp.where(c == 0, brought, kept)
+    g1_o[:, pl.ds(0, 512)] = jnp.where(c == 0, kept, brought)
+    g1_o[:, pl.ds(512, 512)] = jnp.where(c == 0, brought, kept)
 
     link.drain()
 
@@ -783,10 +878,10 @@
     ((768, 1024), BF16), ((1024, 768), BF16), ((768, 512), F32), ((8, 96, 2048), BF16),
     ((4, 96, 512), BF16), ((4, 96, 512), BF16), ((4, 2, 96, 512), BF16),
     ((4, 2, 96, 512), BF16), ((4, 96, 512), BF16), ((96, 2048), F32), ((96, 2048), F32),
-    ((96, 2048), BF16), ((2, 12, 8, 128), F32), ((12, 8, 128), F32), ((8, 96, 2048), BF16),
-    ((768, 1024), F32), ((4, 1024, 512), BF16), ((4, 512, 128), BF16), ((4, 512, 128), BF16),
-    ((4, 2, 512, 128), BF16), ((4, 2, 512, 128), BF16), ((512, 128), BF16),
-    ((512, 128), BF16), ((2, 512, 128), BF16), ((2, 512, 128), BF16), ((768, 512), BF16),
+    ((96, 2048), BF16), ((24, 8, 128), F32), ((12, 8, 128), F32), ((8, 96, 2048), BF16),
+    ((768, 1024), F32), ((4, 1024, 512), BF16), ((4, HALF, 128), BF16), ((4, HALF, 128), BF16),
+    ((4, 2, HALF, 128), BF16), ((4, 2, HALF, 128), BF16), ((HALF, 128), BF16),
+    ((HALF, 128), BF16), ((2, HALF, 128), BF16), ((2, HALF, 128), BF16), ((768, 512), BF16),
     ((768, 512), BF16), ((768, 512), BF16), ((4, 4, 32, 512), BF16), ((4, 16, 512), BF16),
     ((4, 16, 512), BF16), ((2, 4, 16, 512), BF16), ((2, 4, 16, 512), BF16), ((16, 512), BF16),
     ((16, 512), BF16), ((2, 16, 512), BF16), ((2, 16, 512), BF16), ((2, 16, 512), F32),
@@ -794,6 +889,8 @@
     ((3, 3, 8, 128), F32), ((3, 3, 8, 128), F32), ((3, 8, 128), F32), ((3, 8, 128), F32),
     ((3, 8, 128), F32), ((8, 512), BF16), ((8, 384), F32), ((1, 384), jnp.int32),
     ((16, 1024), BF16),
+    ((2, EDGE // 2, 512), BF16), ((2, EDGE // 2, 512), BF16), ((2, EDGE // 2, 512), BF16),
+    ((2, EDGE // 2, 128), BF16), ((2, EDGE // 2, 128), BF16), ((2, EDGE // 2, 128), BF16),
 ]
 
 
@@ -818,7 +915,7 @@
         in_specs=[hbm] * 6 + [smem] * 2,
         out_specs=[vmem] * 5,
         scratch_shapes=[pltpu.VMEM(shape, kind) for shape, kind in SCRATCH]
-        + [pltpu.SemaphoreType.DMA((count,)) for count in (SLOTS, SLOTS, 6)],
+        + [pltpu.SemaphoreType.DMA((count,)) for count in (RING + 18, SLOTS, 6)],
         compiler_params=pltpu.CompilerParams(
             collective_id=0, has_side_effects=True, vmem_limit_bytes=62 * 2**20
         ),

time: 148 us -> 143 us (0.966)
  Pallas kernels: 146 us -> 141 us
    pallas_call x1, Pallas kernels: 144 us -> 139 us  [shards(): pl.pallas_call(kernel, out_shape=[jax.ShapeDtypeStruct(shape, F32) for sh...]
where the time goes in v4:
time: 143 us
  Pallas kernels  141 us (99%)
    pallas_call x1, Pallas kernels, shards(): pl.pallas_call(kernel, out_shape=[jax.ShapeDtypeStruct(shape, F32) for sh...  139 us

profile of v4, /device:TPU:1, one launch (start us, length us, event | category | flops | bytes accessed | tf_op | source)
XLA Modules:
  0.0 142.9 jit_solution(1910180536856232377)
XLA Ops:
  0.6 1.2 reshape.13.number_in
  1.9 138.9 %shard_map.119 = (f32[4,8,128]{2,1,0:T(8,128)}, f32[8,128]{1,0:T(8,128)}, f32[16,1024]{1,0:T(8,128)}, f32[1024,128]{1,0:T(8,128)}, f32[8,512]{1,0:T(8,128)}) custom-call(bf16[384,512]{1,0:T(8,128)(2,1)} %feat.1, bf16[16,1024]{1,0:T(8,128)(2,1)} %w1in.1, bf16[1024,128]{1,0:T(8,128)(2,1)} %w2in.1, bf16[8,512]{1,0:T(8,128)(2,1)} %bitcast.3, ...), custom_call_target="tpu_custom_call" | custom-call | tf_op jit(solution)/shard_map/pallas_call | solution.py:910
  140.8 2.0 %shard_map.120 = (f32[8,384]{1,0:T(8,128)}, f32[1,1]{1,0:T(1,128)}, f32[16,1024]{1,0:T(8,128)}, f32[1024,128]{1,0:T(8,128)}, f32[8,512]{1,0:T(8,128)}) custom-call(f32[4,8,128]{2,1,0:T(8,128)} %get-tuple-element.15.adv, f32[8,128]{1,0:T(8,128)} %get-tuple-element.16.loss, f32[16,1024]{1,0:T(8,128)} %get-tuple-element.17.g1, ...), custom_call_target="tpu_custom_call" | custom-call | tf_op jit(solution)/shard_map/pallas_call | solution.py:926

commit v5 on v4

--- a/solution.py
+++ b/solution.py
@@ -9,7 +9,7 @@
 
 BF16, F32 = jnp.bfloat16, jnp.float32
 MESH = pl.DeviceIdType.MESH
-SLOTS, RING = 195, 64
+SLOTS, RING = 130, 48
 EDGE = 192
 HALF = (1024 - EDGE) // 2
 LOW, HIGH = pl.ds(0, HALF), pl.ds(HALF, HALF)
@@ -56,6 +56,9 @@
         copy.start()
         self.open.append(copy)
         return copy if land is None else self.make(land, land, to, k, 0)
+
+    def all_of(self, ref, k):
+        return self.make(ref, ref, self.peer, k, 0)
 
     def drain(self):
         for copy in self.open[-RING:]:
@@ -86,6 +89,7 @@
         bb = mod(m + step, 16) * 2 + mod(c + dc, 2)
         return bb, mod(zl + dl, 2) * 4 + mod(y + dy, 4)
 
+    link.peer = at(dc=1)
     peers = [(dc, dy, dl) for dc in range(2) for dy in range(4) for dl in range(2)]
 
     loads = [
@@ -97,7 +101,7 @@
                 (feat, F.at[c]),
                 (whin, WHS),
                 (reward_in, RWS),
-                (number_in, EPS),
+                (number_in, EPS.at[0]),
             )
         )
     ]
@@ -124,6 +128,7 @@
     mine, theirs = (
         pl.ds(pl.multiple_of(side * 512, 512), 512) for side in (c, 1 - c)
     )
+    w1_sem = link.take()
     w1pair = push(WIN.at[:, theirs], W1.at[x, zh, c], at(dc=1), W1.at[x, zh, 1 - c])
     W1[x, zh, c] = WIN[:, mine]
 
@@ -136,7 +141,7 @@
         for dx, side in ((1, 0), (3, 1)):
             sides[side].wait_recv()
             part = W1.at[mod(x - dx, 4), zs, side]
-            out.append(push(part, part, at(dx=dx), W1.at[mod(x + 2, 4), zs, side]))
+            out.append(push(part, part, at(dx=dx), k=w1_sem))
         return out
 
     w2x = {}
@@ -186,9 +191,7 @@
         w1far[dz] = w1_across(mod(zh - dz, 4), w1x[dz])
 
     def w1_done():
-        for dz in (0, 1, 3, 2):
-            for copy in w1far[dz]:
-                copy.wait_recv()
+        link.all_of(W1.at[0], w1_sem).wait_recv()
 
     edge = {}
 
@@ -321,12 +324,15 @@
 
     def scatter_a(dz, part=None):
         wide, here = lanes(dz, part)
+        k = link.take()
         came_rs[dz, part] = [
             push(PS.at[over * 2, :, wide], RA.at[dz, :, here], at(dy=1)),
             push(PS.at[over * 2 + 1, :, wide], RB.at[dz, :, here], at(dy=3)),
-            push(PS.at[up * 2 + 1, :, wide], RL.at[dz, 1, :, here], at(dy=1)),
-            push(PS.at[down * 2, :, wide], RR.at[dz, 0, :, here], at(dy=3)),
+            link.all_of(PS.at[pl.ds(0, 4), :, wide], k),
+            k,
         ]
+        push(PS.at[up * 2 + 1, :, wide], RL.at[dz, 1, :, here], at(dy=1), k=k)
+        push(PS.at[down * 2, :, wide], RR.at[dz, 0, :, here], at(dy=3), k=k)
 
     def scatter_b(dz, part=None):
         wide, here = lanes(dz, part)
@@ -337,12 +343,11 @@
             got.wait_recv()
             total = PS[row, :, wide].astype(F32) + buf[dz, :, here].astype(F32)
             PS[row, :, wide] = total.astype(BF16)
-            came_rs[dz, part].append(push(PS.at[row, :, wide], dst, at(dy=dy)))
+            push(PS.at[row, :, wide], dst, at(dy=dy), k=came_rs[dz, part][3])
 
     def scatter_c(dz, part=None):
         wide, here = lanes(dz, part)
-        for got in came_rs[dz, part][2:]:
-            got.wait_recv()
+        came_rs[dz, part][2].wait_recv()
 
         def total(side):
             return (
@@ -512,34 +517,31 @@
     def gather_a(dz, part=None):
         wide, _ = lanes(dz, part)
         src = S.at[r, :, wide]
-        ag[dz, part] = {
-            "pair": push(src, src, at(dl=1), S.at[pair_r, :, wide]),
-            "down": push(src, src, at(dy=1), S.at[down * 2 + zl, :, wide]),
-            "up": push(src, src, at(dy=3), S.at[up * 2 + zl, :, wide]),
-        }
+        k, far = link.take(), link.take()
+        pair = push(src, src, at(dl=1), S.at[pair_r, :, wide])
+        push(src, src, at(dy=1), k=k)
+        push(src, src, at(dy=3), k=k)
+        ag[dz, part] = pair, k, far
 
     def gather_b(dz, part=None):
         wide, _ = lanes(dz, part)
-        got = ag[dz, part]
-        got["pair"].wait_recv()
+        pair, k, _ = ag[dz, part]
+        pair.wait_recv()
         src = S.at[pair_r, :, wide]
-        got["down2"] = push(src, src, at(dy=1), S.at[down * 2 + 1 - zl, :, wide])
-        got["up2"] = push(src, src, at(dy=3), S.at[up * 2 + 1 - zl, :, wide])
+        push(src, src, at(dy=1), k=k)
+        push(src, src, at(dy=3), k=k)
 
     def gather_c(dz, part=None):
         wide, _ = lanes(dz, part)
-        got = ag[dz, part]
-        for name in ("down", "up", "down2", "up2"):
-            got[name].wait_recv()
+        _, k, far = ag[dz, part]
+        link.all_of(S.at[pl.ds(0, 4), :, wide], k).wait_recv()
         low, high = S.at[down * 2, :, wide], S.at[up * 2 + 1, :, wide]
-        got["far"] = [
-            push(low, low, at(dy=1), S.at[over * 2, :, wide]),
-            push(high, high, at(dy=3), S.at[over * 2 + 1, :, wide]),
-        ]
+        push(low, low, at(dy=1), k=far)
+        push(high, high, at(dy=3), k=far)
 
     def gather_d(dz, part=None):
-        for got in ag[dz, part]["far"]:
-            got.wait_recv()
+        wide, _ = lanes(dz, part)
+        link.all_of(S.at[pl.ds(0, 2), :, wide], ag[dz, part][2]).wait_recv()
 
     def grad_part(dz, part):
         wide, here = lanes(dz, part)
@@ -571,11 +573,11 @@
 
     def reduce_far(dz, side):
         src = G2.at[dz, halves[side], lane(2)]
-        gx[dz, side] = [push(src, (XA, XB)[side].at[dz], at(dx=(1, 3)[side]))]
+        gx[dz, side] = push(src, (XA, XB)[side].at[dz], at(dx=(1, 3)[side])), link.take()
 
     def reduce_near(dz, side):
         src = G2.at[dz, halves[side], lane((3, 1)[side])]
-        gx[dz, side].append(push(src, (XR, XL)[side].at[dz, side], at(dx=(3, 1)[side])))
+        push(src, (XR, XL)[side].at[dz, side], at(dx=(3, 1)[side]), k=gx[dz, side][1])
 
     def reduce_a(dz, side):
         reduce_far(dz, side)
@@ -587,12 +589,11 @@
         block = G2[dz, half, lane(dx)].astype(F32) + (XA, XB)[side][dz].astype(F32)
         G2[dz, half, lane(dx)] = block.astype(BF16)
         src = G2.at[dz, half, lane(dx)]
-        gx[dz, side].append(push(src, (XL, XR)[side].at[dz, side], at(dx=dx)))
+        push(src, (XL, XR)[side].at[dz, side], at(dx=dx), k=gx[dz, side][1])
 
     def reduce_c(dz, side, into=None):
         half = halves[side]
-        for got in gx[dz, side][1:]:
-            got.wait_recv()
+        link.all_of(XL.at[dz], gx[dz, side][1]).wait_recv()
         block = (
             G2[dz, half, lane(0)].astype(F32)
             + XL[dz, side].astype(F32)
@@ -603,7 +604,7 @@
         else:
             into[half, :] = block
 
-    e_far, e_in, e_x = [], [], []
+    e_far, e_x, e_sem, ex_sem = [], [], link.take(), link.take()
 
     def edge_far():
         for side in (0, 1):
@@ -612,15 +613,14 @@
 
     def edge_near(dz):
         buf, near, side = (EZL, 1, 0) if dz == 1 else (EZR, 0, 1)
-        e_in.append(push(G2.at[dz, TOPS[near], :], buf.at[near], at(dz=dz)))
+        push(G2.at[dz, TOPS[near], :], buf.at[near], at(dz=dz), k=e_sem)
         e_far[side].wait_recv()
         block = G2[dz, TOPS[side], :].astype(F32) + EZF[side].astype(F32)
         G2[dz, TOPS[side], :] = block.astype(BF16)
-        e_in.append(push(G2.at[dz, TOPS[side], :], buf.at[side], at(dz=dz)))
+        push(G2.at[dz, TOPS[side], :], buf.at[side], at(dz=dz), k=e_sem)
 
     def edge_sum():
-        for got in e_in:
-            got.wait_recv()
+        link.all_of(G2.at[0, pl.ds(0, 2 * EDGE), :], e_sem).wait_recv()
         for side in (0, 1):
             block = (
                 G2[0, TOPS[side], :].astype(F32)
@@ -631,20 +631,19 @@
             src = G2.at[0, TOPS[side]]
             e_x.append(push(src.at[:, lane(2)], EXF.at[side], at(dx=(1, 3)[side])))
             near = (EXR, EXL)[side].at[side]
-            e_x.append(push(src.at[:, lane((3, 1)[side])], near, at(dx=(3, 1)[side])))
+            push(src.at[:, lane((3, 1)[side])], near, at(dx=(3, 1)[side]), k=ex_sem)
 
     def edge_mid():
         for side in (0, 1):
-            e_x[2 * side].wait_recv()
+            e_x[side].wait_recv()
             dx = (1, 3)[side]
             block = G2[0, TOPS[side], lane(dx)].astype(F32) + EXF[side].astype(F32)
             G2[0, TOPS[side], lane(dx)] = block.astype(BF16)
             src = G2.at[0, TOPS[side], lane(dx)]
-            e_x.append(push(src, (EXL, EXR)[side].at[side], at(dx=dx)))
+            push(src, (EXL, EXR)[side].at[side], at(dx=dx), k=ex_sem)
 
     def edge_end():
-        for k in (1, 3, 4, 5):
-            e_x[k].wait_recv()
+        link.all_of(G2.at[0, pl.ds(0, 2 * EDGE), lane(0)], ex_sem).wait_recv()
         for side in (0, 1):
             g2_o[TOPS[side], :] = (
                 G2[0, TOPS[side], lane(0)].astype(F32)
@@ -652,7 +651,7 @@
                 + EXR[side].astype(F32)
             )
 
-    z_far, z_in = [], []
+    z_far, z_sem = [], link.take()
 
     def reduce_z(dz, side):
         half = halves[side]
@@ -664,18 +663,17 @@
             z_far[side].wait_recv()
             block = G2[dz, half, lane(0)].astype(F32) + (ZA, ZB)[side][...].astype(F32)
             G2[dz, half, lane(0)] = block.astype(BF16)
-        z_in.append(push(src, (ZL if dz == 1 else ZR).at[side], at(dz=dz)))
+        push(src, (ZL if dz == 1 else ZR).at[side], at(dz=dz), k=z_sem)
 
     slope_chunk(2)
     gather_a(2, 1)
     gather_a(2, 0)
     slope_chunk(1)
-    gather_a(1)
     slope_chunk(3)
     slope_chunk(0)
     gather_b(2, 1)
     gather_b(2, 0)
-    gather_a(3)
+    gather_a(1)
 
     for i in range(4):
         adv_o[i] = ADV[4 * c + i]
@@ -690,8 +688,8 @@
         GHP[g, 2] = own_loss
     gather_c(2, 1)
     gather_c(2, 0)
+    gather_a(3)
     gather_b(1)
-    gather_a(0)
     gh_sem, gh_all = link.take(), GR.at[pl.ds(0, 7)]
     for dc, dy, dl in peers[1:8]:
         to_j = mod(zl + dl, 2) * 4 + mod(y + dy, 4)
@@ -709,10 +707,11 @@
     edge_far()
     gather_c(1)
     gather_b(3)
-    gather_b(0)
+    gather_a(0)
     back_first(2, True)
     reduce_b(2, 0)
     reduce_b(2, 1)
+    gather_b(0)
     gather_d(1)
     grad_second(1, 1)
     reduce_a(1, 1)
@@ -766,9 +765,10 @@
     yin = [
         push(G1.at[x2, :, lo], YA, at(dx=1)),
         push(G1.at[x2, :, hi], YB, at(dx=3)),
-        push(G1.at[x1, :, hi], YL.at[1], at(dx=1)),
-        push(G1.at[x3, :, lo], YR.at[0], at(dx=3)),
     ]
+    y_sem, u_sem = link.take(), link.take()
+    push(G1.at[x1, :, hi], YL.at[1], at(dx=1), k=y_sem)
+    push(G1.at[x3, :, lo], YR.at[0], at(dx=3), k=y_sem)
     reduce_b(3, 1)
     grad_second(0, 1)
     reduce_c(1, 1)
@@ -786,7 +786,7 @@
             got.wait_recv()
             block = G1[row, :, half].astype(F32) + buf[...].astype(F32)
             G1[row, :, half] = block.astype(BF16)
-            yin.append(push(G1.at[row, :, half], dst, at(dx=dx)))
+            push(G1.at[row, :, half], dst, at(dx=dx), k=y_sem)
 
     sums_y()
     reduce_a(0, 0)
@@ -801,17 +801,16 @@
     gz_in = [link.make(GZ, GZ, at(dz=1), gz_sem, 0)]
     reduce_c(3, 1)
     reduce_z(3, 1)
-    for got in yin[2:]:
-        got.wait_recv()
+    link.all_of(G1.at[pl.ds(0, 2)], y_sem).wait_recv()
     for side, half in ((0, lo), (1, hi)):
         block = G1[x, :, half].astype(F32) + YL[side].astype(F32) + YR[side].astype(F32)
         G1[x, :, half] = block.astype(BF16)
     uin = [
         push(G1.at[x, z2, lo], UA, at(dz=1)),
         push(G1.at[x, z2, hi], UB, at(dz=3)),
-        push(G1.at[x, z1, hi], UL.at[1], at(dz=1)),
-        push(G1.at[x, z3, lo], UR.at[0], at(dz=3)),
     ]
+    push(G1.at[x, z1, hi], UL.at[1], at(dz=1), k=u_sem)
+    push(G1.at[x, z3, lo], UR.at[0], at(dz=3), k=u_sem)
     reduce_b(0, 0)
     reduce_b(0, 1)
     edge_mid()
@@ -822,7 +821,7 @@
         got.wait_recv()
         block = G1[x, row, half].astype(F32) + buf[...].astype(F32)
         G1[x, row, half] = block.astype(BF16)
-        uin.append(push(G1.at[x, row, half], dst, at(dz=dz)))
+        push(G1.at[x, row, half], dst, at(dz=dz), k=u_sem)
     for got in gz_in:
         got.wait_recv()
     GY[...] = GS[...] + GZ[0] + GZ[1] + GZ[2]
@@ -834,8 +833,7 @@
     heads = GY[...] + GX[0] + GX[1] + GX[2]
     GH[...] = heads
     gc_in = push(GH, GC, at(dc=1))
-    for got in uin[2:]:
-        got.wait_recv()
+    link.all_of(G1.at[0, pl.ds(0, 2)], u_sem).wait_recv()
     for side, half in ((0, lo), (1, hi)):
         GF[side] = (
             G1[x, zh, half].astype(F32) + UL[side].astype(F32) + UR[side].astype(F32)
@@ -850,8 +848,7 @@
     reduce_c(0, 0, g2_o)
     reduce_c(0, 1, g2_o)
     edge_end()
-    for got in z_in:
-        got.wait_recv()
+    link.all_of(XL.at[pl.ds(0, 2)], z_sem).wait_recv()
     for side, half in ((0, LOW), (1, HIGH)):
         g2_o[half, :] = g2_o[half, :] + ZL[side].astype(F32) + ZR[side].astype(F32)
     gt_in.wait_recv()
@@ -920,7 +917,7 @@
             collective_id=0, has_side_effects=True, vmem_limit_bytes=62 * 2**20
         ),
     )(
-        features, w_first, w_second, w_head.T, rewards, episode.reshape(1, -1),
+        features, w_first, w_second, w_head.T, rewards, episode,
         discount, trace,
     )
     advantages, loss, grad_first, grad_second, grad_head = pl.pallas_call(

time: 143 us -> 140 us (0.979)
  Pallas kernels: 141 us -> 139 us
    pallas_call x1, Pallas kernels: 139 us -> 137 us  [shards(): pl.pallas_call(kernel, out_shape=[jax.ShapeDtypeStruct(shape, F32) for sh...]
where the time goes in v5:
time: 140 us
  Pallas kernels  139 us (99%)
    pallas_call x1, Pallas kernels, shards(): pl.pallas_call(kernel, out_shape=[jax.ShapeDtypeStruct(shape, F32) for sh...  137 us

profile of v5, /device:TPU:1, one launch (start us, length us, event | category | flops | bytes accessed | tf_op | source)
XLA Modules:
  0.0 140.1 jit_solution(12187244019963528494)
XLA Ops:
  0.6 137.4 %shard_map.119 = (f32[4,8,128]{2,1,0:T(8,128)}, f32[8,128]{1,0:T(8,128)}, f32[16,1024]{1,0:T(8,128)}, f32[1024,128]{1,0:T(8,128)}, f32[8,512]{1,0:T(8,128)}) custom-call(bf16[384,512]{1,0:T(8,128)(2,1)} %feat.1, bf16[16,1024]{1,0:T(8,128)(2,1)} %w1in.1, bf16[1024,128]{1,0:T(8,128)(2,1)} %w2in.1, bf16[8,512]{1,0:T(8,128)(2,1)} %bitcast.3, ...), custom_call_target="tpu_custom_call" | custom-call | tf_op jit(solution)/shard_map/pallas_call | solution.py:907
  138.0 2.0 %shard_map.120 = (f32[8,384]{1,0:T(8,128)}, f32[1,1]{1,0:T(1,128)}, f32[16,1024]{1,0:T(8,128)}, f32[1024,128]{1,0:T(8,128)}, f32[8,512]{1,0:T(8,128)}) custom-call(f32[4,8,128]{2,1,0:T(8,128)} %get-tuple-element.15.adv, f32[8,128]{1,0:T(8,128)} %get-tuple-element.16.loss, f32[16,1024]{1,0:T(8,128)} %get-tuple-element.17.g1, ...), custom_call_target="tpu_custom_call" | custom-call | tf_op jit(solution)/shard_map/pallas_call | solution.py:923

commit v6 on v5

--- a/solution.py
+++ b/solution.py
@@ -9,7 +9,7 @@
 
 BF16, F32 = jnp.bfloat16, jnp.float32
 MESH = pl.DeviceIdType.MESH
-SLOTS, RING = 130, 48
+SLOTS, RING = 130, 32
 EDGE = 192
 HALF = (1024 - EDGE) // 2
 LOW, HIGH = pl.ds(0, HALF), pl.ds(HALF, HALF)
@@ -114,15 +114,8 @@
     partners += [beside(step, *peer) for step in (1, -1) for peer in peers]
     for partner in partners:
         pl.semaphore_signal(barrier, inc=1, device_id=partner, device_id_type=MESH)
-    for load in loads:
+    for load in loads[:3]:
         load.wait()
-    blank = jnp.zeros((8, 32), F32)
-    WHB[j] = WHS[...].astype(F32)
-    for i in range(4):
-        reward = RWS[:, i * 96 : (i + 1) * 96]
-        number = jnp.broadcast_to(EPS[:, i * 96 : (i + 1) * 96].astype(F32), (8, 96))
-        RE[c, 0, i] = jnp.concatenate([reward, blank], axis=1)
-        RE[c, 1, i] = jnp.concatenate([number, blank], axis=1)
     pl.semaphore_wait(barrier, len(partners))
 
     mine, theirs = (
@@ -236,6 +229,15 @@
     edge_x2()
     w1_from_z(2)
     second += [w2_z(HIGH, 1), w2_z(LOW, 3)]
+    for load in loads[3:]:
+        load.wait()
+    blank = jnp.zeros((8, 32), F32)
+    WHB[j] = WHS[...].astype(F32)
+    for i in range(4):
+        reward = RWS[:, i * 96 : (i + 1) * 96]
+        number = jnp.broadcast_to(EPS[:, i * 96 : (i + 1) * 96].astype(F32), (8, 96))
+        RE[c, 0, i] = jnp.concatenate([reward, blank], axis=1)
+        RE[c, 1, i] = jnp.concatenate([number, blank], axis=1)
     re_in = push(RE.at[c], RE.at[c], at(dc=1), RE.at[1 - c])
     re_sem = link.take()
     re_to = [
@@ -559,6 +561,15 @@
             size = (HALF if side == 0 else HALF + EDGE) // 2
             rows = pl.ds(pl.multiple_of(side * HALF + n * size, 16), size)
             G2[dz, rows, :] = dot(HFT[rows, :], S[:, :, at_dz].reshape(768, 512)).astype(BF16)
+
+    def back_half(dz, side):
+        at_dz = pl.ds(dz * 512, 512)
+
+        @pl.loop(0, 2)
+        def _(n):
+            cols = pl.ds(pl.multiple_of(side * 512 + n * 256, 256), 256)
+            part = dot(S[:, :, at_dz].reshape(768, 512), W2[dz, cols, :], ((1,), (1,)))
+            BACK[:, cols] = BACK[:, cols] + part
 
     def back_first(dz, start):
         at_dz = pl.ds(dz * 512, 512)
@@ -719,6 +730,13 @@
     reduce_a(1, 0)
     gather_c(3)
     back_first(1, False)
+    for got in gh_in:
+        got.wait_recv()
+    GS[...] = functools.reduce(jnp.add, [GR[i] for i in range(8)])
+    gz_sem, gx_sem = link.take(), link.take()
+    for d in (1, 2, 3):
+        push(GS, GZ.at[d - 1], at(dz=d), k=gz_sem)
+    gz_in = [link.make(GZ, GZ, at(dz=1), gz_sem, 0)]
     edge_near(1)
     gather_c(0)
     reduce_b(1, 1)
@@ -735,7 +753,7 @@
     reduce_z(2, 1)
     back_first(3, False)
     gather_d(0)
-    back_first(0, False)
+    back_half(0, 1 - c)
 
     @pl.loop(0, 12)
     def _(i):
@@ -743,6 +761,7 @@
         BKS[rows, :] = BACK[rows, theirs].astype(BF16)
 
     back_in = push(BKS, BKR, at(dc=1))
+    back_half(0, c)
     reduce_b(3, 0)
     grad_second(0, 0)
     back_in.wait_recv()
@@ -771,6 +790,12 @@
     push(G1.at[x3, :, lo], YR.at[0], at(dx=3), k=y_sem)
     reduce_b(3, 1)
     grad_second(0, 1)
+    for got in gz_in:
+        got.wait_recv()
+    GY[...] = GS[...] + GZ[0] + GZ[1] + GZ[2]
+    for d in (1, 2, 3):
+        push(GY, GX.at[d - 1], at(dx=d), k=gx_sem)
+    gxs_in = [link.make(GX, GX, at(dx=1), gx_sem, 0)]
     reduce_c(1, 1)
     reduce_z(1, 1)
     reduce_c(1, 0)
@@ -792,13 +817,11 @@
     reduce_a(0, 0)
     reduce_a(0, 1)
     edge_sum()
-    for got in gh_in:
+    for got in gxs_in:
         got.wait_recv()
-    GS[...] = functools.reduce(jnp.add, [GR[i] for i in range(8)])
-    gz_sem, gx_sem = link.take(), link.take()
-    for d in (1, 2, 3):
-        push(GS, GZ.at[d - 1], at(dz=d), k=gz_sem)
-    gz_in = [link.make(GZ, GZ, at(dz=1), gz_sem, 0)]
+    heads = GY[...] + GX[0] + GX[1] + GX[2]
+    GH[...] = heads
+    gc_in = push(GH, GC, at(dc=1))
     reduce_c(3, 1)
     reduce_z(3, 1)
     link.all_of(G1.at[pl.ds(0, 2)], y_sem).wait_recv()
@@ -822,17 +845,6 @@
         block = G1[x, row, half].astype(F32) + buf[...].astype(F32)
         G1[x, row, half] = block.astype(BF16)
         push(G1.at[x, row, half], dst, at(dz=dz), k=u_sem)
-    for got in gz_in:
-        got.wait_recv()
-    GY[...] = GS[...] + GZ[0] + GZ[1] + GZ[2]
-    for d in (1, 2, 3):
-        push(GY, GX.at[d - 1], at(dx=d), k=gx_sem)
-    gxs_in = [link.make(GX, GX, at(dx=1), gx_sem, 0)]
-    for got in gxs_in:
-        got.wait_recv()
-    heads = GY[...] + GX[0] + GX[1] + GX[2]
-    GH[...] = heads
-    gc_in = push(GH, GC, at(dc=1))
     link.all_of(G1.at[0, pl.ds(0, 2)], u_sem).wait_recv()
     for side, half in ((0, lo), (1, hi)):
         GF[side] = (

time: 140 us -> 140 us (level)
  no operation moved by 1% of the time
where the time goes in v6:
time: 140 us; the launch traced here: 139 us
  Pallas kernels  139 us (99%)
    pallas_call x1, Pallas kernels, shards(): pl.pallas_call(kernel, out_shape=[jax.ShapeDtypeStruct(shape, F32) for sh...  137 us

profile of v6, /device:TPU:1, one launch (start us, length us, event | category | flops | bytes accessed | tf_op | source)
XLA Modules:
  0.0 139.5 jit_solution(12606414978957576410)
XLA Ops:
  0.6 136.7 %shard_map.119 = (f32[4,8,128]{2,1,0:T(8,128)}, f32[8,128]{1,0:T(8,128)}, f32[16,1024]{1,0:T(8,128)}, f32[1024,128]{1,0:T(8,128)}, f32[8,512]{1,0:T(8,128)}) custom-call(bf16[384,512]{1,0:T(8,128)(2,1)} %feat.1, bf16[16,1024]{1,0:T(8,128)(2,1)} %w1in.1, bf16[1024,128]{1,0:T(8,128)(2,1)} %w2in.1, bf16[8,512]{1,0:T(8,128)(2,1)} %bitcast.3, ...), custom_call_target="tpu_custom_call" | custom-call | tf_op jit(solution)/shard_map/pallas_call | solution.py:919
  137.4 2.0 %shard_map.120 = (f32[8,384]{1,0:T(8,128)}, f32[1,1]{1,0:T(1,128)}, f32[16,1024]{1,0:T(8,128)}, f32[1024,128]{1,0:T(8,128)}, f32[8,512]{1,0:T(8,128)}) custom-call(f32[4,8,128]{2,1,0:T(8,128)} %get-tuple-element.15.adv, f32[8,128]{1,0:T(8,128)} %get-tuple-element.16.loss, f32[16,1024]{1,0:T(8,128)} %get-tuple-element.17.g1, ...), custom_call_target="tpu_custom_call" | custom-call | tf_op jit(solution)/shard_map/pallas_call | solution.py:935
